TPU v7x, 32 devices: a whole 2x2x4 slice. The times are simulated.
32 devices in a mesh: data: 32 (over z, y, x, core).
Axes of the slice: x: 2, y: 2, z: 4, core: 2. Of those that a mesh axis runs over, the one named last changes fastest.
Arguments:
- view_one: bfloat16 [2048, 256], P('data')
- view_two: bfloat16 [2048, 256], P('data')
- protos: bfloat16 [8192, 256], replicated
- valid_mask: int32 [2048], P('data')
Outputs:
- output 1: float32 [2048, 8192], P('data')
- output 2: float32 [2048, 8192], P('data')
- output 3: float32 [], replicated
- output 4: float32 [2048, 256], P('data')
- output 5: float32 [2048, 256], P('data')
- output 6: float32 [8192, 256], replicated
All inputs are finite; a program needn't handle non-finite values.
Results may differ from a plain program's by a relative error of at most 0.001.
Values are sent between devices in bfloat16 or wider.
A program may use at most 1 GiB of HBM per device.

v0:
```python
import jax
import jax.numpy as jnp
from jax import lax
from jax.sharding import PartitionSpec as P

SINK_EPS = 0.05
SOFT_TEMP = 0.1
SINK_ITERS = 3


def solution(mesh):
    def value_a14(scores, weights, valid_count):
        proto_count = scores.shape[1]
        transport = jnp.exp(scores / SINK_EPS) * weights
        for sweep_idx in range(SINK_ITERS):
            col_sum = lax.psum(jnp.sum(transport, axis=0, keepdims=True), "data")
            transport = transport / (proto_count * col_sum)
            row_sum = jnp.sum(transport, axis=1, keepdims=True) + (1.0 - weights)
            transport = transport / (valid_count * row_sum)
        return transport * valid_count

    def local_step(view_one, view_two, protos, valid_mask):
        weights = valid_mask.astype(jnp.float32)[:, None]
        valid_count = lax.psum(jnp.sum(weights), "data")
        score_one = jnp.einsum("nd,kd->nk", view_one, protos, preferred_element_type=jnp.float32)
        codes_one = value_a14(score_one, weights, valid_count)
        score_two = jnp.einsum("nd,kd->nk", view_two, protos, preferred_element_type=jnp.float32)
        codes_two = value_a14(score_two, weights, valid_count)
        logp_one = jax.nn.log_softmax(score_one / SOFT_TEMP, axis=1)
        logp_two = jax.nn.log_softmax(score_two / SOFT_TEMP, axis=1)
        part_loss = -(jnp.sum(codes_two * logp_one) + jnp.sum(codes_one * logp_two))
        loss_value = lax.psum(part_loss, "data") / (2.0 * valid_count)
        grad_scale = weights / (2.0 * valid_count * SOFT_TEMP)
        grad_one = ((jnp.exp(logp_one) - codes_two) * grad_scale).astype(jnp.bfloat16)
        grad_two = ((jnp.exp(logp_two) - codes_one) * grad_scale).astype(jnp.bfloat16)
        dz_one = jnp.dot(grad_one, protos, preferred_element_type=jnp.float32)
        dz_two = jnp.dot(grad_two, protos, preferred_element_type=jnp.float32)
        part_grad = (jnp.einsum("nk,nd->kd", grad_one, view_one, preferred_element_type=jnp.float32)
                     + jnp.einsum("nk,nd->kd", grad_two, view_two, preferred_element_type=jnp.float32))
        d_protos = lax.psum(part_grad, "data")
        return codes_one, codes_two, loss_value, dz_one, dz_two, d_protos

    return jax.shard_map(
        local_step,
        mesh=mesh,
        in_specs=(P("data", None), P("data", None), P(None, None), P("data")),
        out_specs=(P("data", None), P("data", None), P(), P("data", None), P("data", None), P(None, None)),
        check_vma=False,
    )
```

profile of v0, /device:TPU:0, one launch (start us, length us, event | category | flops | bytes accessed | tf_op | source)
XLA Modules:
  0.0 534.1 jit_solution(14861965606781530054)
XLA Ops:
  7.2 1.3 convert_reduce_fusion
  8.5 0.7 convert_element_type.9
  9.1 5.2 multiply_reduce_fusion.2
  14.3 1.5 multiply_reduce_fusion.3
  15.9 42.5 %all-reduce.1 = (f32[]{:T(128)}, f32[1,8192]{1,0:T(1,128)S(1)}) all-reduce(f32[]{:T(128)} %convert_reduce_fusion, f32[1,8192]{1,0:T(1,128)S(1)} %bitcast.50), channel_id=1, replica_groups=mesh['data'=32] {'data'}, use_global_device_ids=true, to_apply=%region_3.0 | all-reduce | flops 8193 | bytes 65544 | tf_op jit(solution)/shard_map/psum | solution.py:24
  58.4 0.9 exponential_reduce_fusion.1
  60.0 2.0 exponential_reduce_fusion
  62.0 40.3 %psum.65 = f32[1,8192]{1,0:T(1,128)S(1)} all-reduce(f32[1,8192]{1,0:T(1,128)S(1)} %bitcast.51), channel_id=1, replica_groups=mesh['data'=32] {'data'}, use_global_device_ids=true, to_apply=%region_6.0 | all-reduce | flops 8192 | bytes 65536 | tf_op jit(solution)/shard_map/psum | solution.py:16
  102.3 0.7 fusion.19
  103.7 1.4 fusion.20
  106.0 127.8 %all-reduce.7.cloned.1.call-done = (f32[1,8192]{1,0:T(1,128)}, f32[1,8192]{1,0:T(1,128)}) async-done(((f32[1,8192]{1,0:T(1,128)}, f32[1,8192]{1,0:T(1,128)}), (f32[1,8192]{1,0:T(1,128)}, f32[1,8192]{1,0:T(1,128)})) %all-reduce.7.cloned.1.call-update) | async-done | bytes 65552 | tf_op jit(solution)/shard_map/psum | solution.py:16
  233.9 1.0 broadcast_multiply_fusion.2
  234.9 0.9 fusion.23
  235.8 0.7 add_multiply_fusion.3
  236.4 3.2 multiply_convert_fusion
  239.6 1.7 multiply_reduce_fusion
  242.7 39.4 %psum.68 = f32[1,8192]{1,0:T(1,128)S(1)} all-reduce(f32[1,8192]{1,0:T(1,128)S(1)} %bitcast.52), channel_id=1, replica_groups=mesh['data'=32] {'data'}, use_global_device_ids=true, to_apply=%region_15.0 | all-reduce | flops 8192 | bytes 65536 | tf_op jit(solution)/shard_map/psum | solution.py:16
  282.2 2.5 fusion.18
  284.6 0.7 add_multiply_fusion.1
  285.3 0.8 fusion.21
  286.1 40.2 %psum.69 = f32[1,8192]{1,0:T(1,128)S(1)} all-reduce(f32[1,8192]{1,0:T(1,128)S(1)} %bitcast.53), channel_id=1, replica_groups=mesh['data'=32] {'data'}, use_global_device_ids=true, to_apply=%region_18.0 | all-reduce | flops 8192 | bytes 65536 | tf_op jit(solution)/shard_map/psum | solution.py:16
  326.4 2.6 fusion.22
  329.0 0.7 add_multiply_fusion
  329.7 3.4 multiply_convert_fusion.1
  333.1 1.3 fusion.30
  334.4 4.7 convolution_add_fusion
  339.2 2.9 multiply_reduce_fusion.1
  344.0 41.3 %psum.70 = f32[]{:T(128)} all-reduce(f32[]{:T(128)S(6)} %neg.3), channel_id=1, replica_groups=mesh['data'=32] {'data'}, use_global_device_ids=true, to_apply=%region_24.0 | all-reduce | flops 1 | bytes 8 | tf_op jit(solution)/shard_map/psum | solution.py:32
  386.0 4.1 fusion.29
  390.1 1.4 fusion.28
  391.5 127.3 %all-reduce.5.cloned.1.call-done = f32[8192,256]{1,0:T(8,128)} async-done(((f32[8192,256]{1,0:T(8,128)}), f32[8192,256]{1,0:T(8,128)}) %all-reduce.5.cloned.1.call-update) | async-done | bytes 8388624 | tf_op jit(solution)/shard_map/psum | solution.py:40
  518.8 7.3 %copy.13 = f32[8192,256]{1,0:T(8,128)} copy(f32[8192,256]{1,0:T(8,128)} %all-reduce.5.cloned.1.call-done) | data formatting | bytes 16777216
  (36 shorter events, 3.1 us)
Async XLA Ops:
  7.2 7.2 %copy-start = (bf16[64,256]{1,0:T(8,128)(2,1)S(1)}, bf16[64,256]{1,0:T(8,128)(2,1)}, u32[]{:S(2)}) copy-start(bf16[64,256]{1,0:T(8,128)(2,1)} %param.5) | copy-start | bytes 98308
  7.2 226.7 %all-reduce.7.cloned.1.call-start = ((), (), s32[]{:S(2)}) async-start(), calls=%async_computation.1 | async-start | bytes 131072 | tf_op jit(solution)/shard_map/psum | solution.py:16
  9.1 5.2 copy-start.5
  15.9 43.5 %copy-start.10 = (s32[64]{0:T(128)S(1)}, s32[64]{0:T(128)}, u32[]{:S(2)}) copy-start(s32[64]{0:T(128)} %param.8) | copy-start | bytes 772
  58.3 1.6 copy-start.1
  105.1 413.6 %all-reduce.5.cloned.1.call-start = ((), (), s32[]{:S(2)}) async-start(), calls=%async_computation | async-start | bytes 16777216 | tf_op jit(solution)/shard_map/psum | solution.py:40
  233.9 2.5 copy-start.2
  239.6 1.8 copy-start.8
  282.1 3.2 copy-start.3
  326.3 3.3 copy-start.4
  333.1 1.3 copy-start.7
  333.1 1.3 copy-start.9
  386.0 4.1 copy-start.6
Sparse Core Ops, SparseCore 0:
  105.3 128.5 all-reduce.6
  339.3 179.4 all-reduce.4
where the time goes:
time: 535 us; the launch traced here: 534 us
  waiting for transfers between devices  255 us (48%)
  blocking collectives  204 us (38%)
  other arithmetic  30.8 us (6%)
  between operations  18.7 us (3%)
  matrix products  18.2 us (3%)
  local copies, waits for them, and re-layouts  7.38 us (1%)
    psum x1, waiting for transfers between devices, value_a14(): col_sum = lax.psum(jnp.sum(transport, axis=0, keepdims=True), 'data')  128 us
    psum x1, waiting for transfers between devices, local_step(): d_protos = lax.psum(part_grad, 'data')  127 us
    psum x3, blocking collectives, value_a14(): col_sum = lax.psum(jnp.sum(transport, axis=0, keepdims=True), 'data')  120 us
    psum x1, blocking collectives, local_step(): valid_count = lax.psum(jnp.sum(weights), 'data')  42.5 us
    psum x1, blocking collectives, local_step(): loss_value = lax.psum(part_loss, 'data') / (2.0 * valid_count)  41.3 us
  transfers between devices with their start and end apart: 2, of which 2 were waited for; matrix products, arithmetic and copies ran while one was open for 2% of the time, Pallas kernels for 0%

commit v1 on v0

v1 whole, which is shorter than its diff:
```python
import jax
import jax.numpy as jnp
from jax import lax
from jax.experimental import pallas as pl
from jax.experimental.pallas import tpu as pltpu
from jax.sharding import PartitionSpec as P

MESH = pl.DeviceIdType.MESH
F32 = jnp.float32
BF16 = jnp.bfloat16

ROWS = 64
DEVS = 32
PLANE = 8
SAMPLES = ROWS * DEVS
PROTOS = 8192
DIM = 256
COLS = PROTOS // PLANE
ITERS = 3
INV_T = 10.0
SLAB = 2 * ROWS + 16
UNIT = 64
UNITS = COLS // UNIT
DIRECT = 11
NT = (((1,), (1,)), ((), ()))


def kernel(v1_hbm, v2_hbm, mk_hbm, c_hbm,
           q1_ref, q2_ref, loss_ref, dz1_ref, dz2_ref, dc_ref,
           zc, call, e_ref, vbc, mden, uden, ub, rbuf, vall, lbuf, lzbuf, colv,
           lsem, z_send, z_recv, ar_send, ar_recv, v_send, v_recv,
           l_send, l_recv, lz_send, lz_recv,
           d_recv, dcore_recv, d_sf, d_ss, d_sc, d_fs, d_sz):
    me = lax.axis_index("data")
    z = me // PLANE
    j = me % PLANE
    c = j % 2
    x = (j // 2) % 2
    y = j // 4
    jx = j + 2 - 4 * x
    jy = j + 4 - 8 * y
    jd = (6 - 2 * (j // 2)) + c
    jf = jx + c * (jy - jx)
    js = jy + c * (jx - jy)
    core = me + 1 - 2 * c
    first = z * PLANE + jf
    second = z * PLANE + js
    par = z % 2
    zpart = me + PLANE - 2 * PLANE * par

    barrier = pltpu.get_barrier_semaphore()
    for t in range(1, PLANE):
        pl.semaphore_signal(barrier, inc=1, device_id=(z * PLANE + (j + t) % PLANE,), device_id_type=MESH)
    for t in range(1, 4):
        pl.semaphore_signal(barrier, inc=1, device_id=(((z + t) % 4) * PLANE + j,), device_id_type=MESH)

    own = [
        pltpu.make_async_copy(v1_hbm, zc.at[me, pl.ds(0, ROWS), :], lsem.at[0]),
        pltpu.make_async_copy(v2_hbm, zc.at[me, pl.ds(ROWS, ROWS), :], lsem.at[1]),
        pltpu.make_async_copy(mk_hbm, zc.at[me, pl.ds(2 * ROWS, 16), :], lsem.at[2]),
    ]
    for cp in own:
        cp.start()
    c_copy = pltpu.make_async_copy(c_hbm, call, lsem.at[3])
    c_copy.start()
    for cp in own:
        cp.wait()
    pl.semaphore_wait(barrier, PLANE - 1 + 3)

    def remote(src, dst, ssem, rsem, dev):
        return pltpu.make_async_remote_copy(src_ref=src, dst_ref=dst, send_sem=ssem, recv_sem=rsem,
                                            device_id=(dev,), device_id_type=MESH)

    pending = []

    def z_copy(i, dev):
        cp = remote(zc.at[i], zc.at[i], z_send.at[len(pending)], z_recv.at[i], dev)
        pending.append(cp)
        cp.start()

    def z_wait(i):
        remote(zc.at[i], zc.at[i], z_send.at[0], z_recv.at[i], me).wait_recv()

    def rel(t):
        return ((z + t) % 4) * PLANE

    z_copy(me, first)
    z_copy(me, second)
    for t in range(1, 4):
        z_copy(me, rel(t) + j)
    z_copy(me, core)

    def take_f(t):
        z_wait(rel(t) + jf)
        z_copy(rel(t) + jf, second)
        z_copy(rel(t) + jf, core)

    def take_s(t):
        z_wait(rel(t) + js)
        z_copy(rel(t) + js, core)
        z_wait(rel(t) + jd)
        z_copy(rel(t) + jd, core)

    def take_core(t):
        for q in range(4):
            z_wait(rel(t) + 2 * q + 1 - c)

    take_f(0)
    for t in range(1, 4):
        z_wait(rel(t) + j)
        z_copy(rel(t) + j, first)
        z_copy(rel(t) + j, second)
        z_copy(rel(t) + j, core)
    take_s(0)
    for t in range(1, 4):
        take_f(t)
    take_s(1)
    c_copy.wait()

    def scores(t):
        p = (z + t) % 4
        for v in range(2):
            zb = zc[pl.ds(p * PLANE, PLANE), v * ROWS:(v + 1) * ROWS, :].reshape(PLANE * ROWS, DIM)

            def body(kb, acc, v=v, zb=zb):
                cs = call[pl.ds(pl.multiple_of(j * COLS + kb * 128, 128), 128), :]
                s = lax.dot_general(cs, zb, NT, preferred_element_type=F32)
                e = jnp.exp(s * INV_T)
                e_ref[v, pl.ds(pl.multiple_of(kb * 128, 128), 128), pl.ds(pl.multiple_of(p * 512, 512), 512)] = e
                return acc + jnp.sum(e.reshape(16, 8, 512), axis=0)

            acc = lax.fori_loop(0, COLS // 128, body, jnp.zeros((8, 512), F32))
            tot = jnp.sum(acc, axis=0, keepdims=True)
            for b in range(4):
                rbuf[0, j, pl.ds(v * 16 + p * 4 + b, 1), :] = tot[:, b * 128:(b + 1) * 128]

    take_core(0)
    scores(0)
    take_s(2)
    take_core(1)
    scores(1)
    take_s(3)
    take_core(2)
    scores(2)
    take_core(3)
    scores(3)

    def ar_copies(ph):
        return [remote(rbuf.at[ph, j], rbuf.at[ph, j], ar_send.at[ph, t - 1], ar_recv.at[ph, j],
                       z * PLANE + (j + t) % PLANE) for t in range(1, PLANE)]

    def ar_wait(ph):
        for t in range(1, PLANE):
            o = (j + t) % PLANE
            remote(rbuf.at[ph, o], rbuf.at[ph, o], ar_send.at[ph, 0], ar_recv.at[ph, o], me).wait_recv()

    def ar_sum(ph):
        tot = rbuf[ph, 0]
        for o in range(1, PLANE):
            tot = tot + rbuf[ph, o]
        return tot

    for cp in ar_copies(0):
        cp.start()

    lane = lax.broadcasted_iota(jnp.int32, (1, 128), 1)
    for b in range(16):
        even = zc[2 * b, 2 * ROWS:2 * ROWS + 16, 0:128].astype(F32)[0:1]
        odd = zc[2 * b + 1, 2 * ROWS:2 * ROWS + 16, 0:128].astype(F32)[0:1]
        mrow = jnp.where(lane < ROWS, even, odd)
        mden[pl.ds(b, 1), :] = mrow
        mden[pl.ds(16 + b, 1), :] = mrow
    valid = jnp.sum(jnp.sum(mden[0:16, :], axis=0, keepdims=True), axis=1, keepdims=True)

    def spread(dense, slot):
        uden[...] = dense
        for v in range(2):
            for b in range(16):
                ub[slot, v, :, b * 128:(b + 1) * 128] = jnp.broadcast_to(uden[pl.ds(v * 16 + b, 1), :], (8, 128))

    spread(mden[...], 0)

    KB = 32

    def sweep(ph):
        for v in range(2):
            u = ub[0, v]

            def rows(kb):
                w = e_ref[v, pl.ds(pl.multiple_of(kb * KB, KB), KB), :]
                return (w * w).reshape(KB // 8, 8, SAMPLES)

            def body(kb, carry):
                acc, vprev = carry
                wu = rows(kb) * u[None]
                part = wu[:, :, 0:128]
                for b in range(1, 16):
                    part = part + wu[:, :, b * 128:(b + 1) * 128]
                col = jnp.sum(part.reshape(KB, 128), axis=1, keepdims=True)
                vnew = jnp.broadcast_to(1.0 / (PROTOS * col), (KB, 128))
                vbc[v, pl.ds(pl.multiple_of(kb * KB, KB), KB), :] = vnew
                old = rows(jnp.maximum(kb - 1, 0))
                vb = jnp.concatenate([vprev.reshape(KB // 8, 8, 128)] * 16, axis=2)
                acc = acc + jnp.sum(old * vb, axis=0)
                return acc, vnew

            acc, vlast = lax.fori_loop(0, COLS // KB, body, (jnp.zeros((8, SAMPLES), F32), jnp.zeros((KB, 128), F32)))
            vb = jnp.concatenate([vlast.reshape(KB // 8, 8, 128)] * 16, axis=2)
            acc = acc + jnp.sum(rows(COLS // KB - 1) * vb, axis=0)
            tot = jnp.sum(acc, axis=0, keepdims=True)
            for b in range(16):
                rbuf[ph, j, pl.ds(v * 16 + b, 1), :] = tot[:, b * 128:(b + 1) * 128]

    v_copies = []
    u3 = None
    for it in range(ITERS):
        ph = it + 1
        sweep(ph)
        for cp in ar_copies(ph):
            cp.start()
        if it == 0:
            ar_wait(0)
        if it == ITERS - 1:
            diag = (lax.broadcasted_iota(jnp.int32, (128, 128), 0) == lax.broadcasted_iota(jnp.int32, (128, 128), 1))
            for v in range(2):
                for b in range(COLS // 128):
                    blk = vbc[v, b * 128:(b + 1) * 128, :]
                    vall[j, pl.ds(v, 1), b * 128:(b + 1) * 128] = jnp.sum(jnp.where(diag, blk, 0.0), axis=0, keepdims=True)
            v_copies = [remote(vall.at[j], vall.at[j], v_send.at[t - 1], v_recv.at[j],
                               z * PLANE + (j + t) % PLANE) for t in range(1, PLANE)]
            for cp in v_copies:
                cp.start()
        ar_wait(ph)
        u3 = mden[...] / (valid * ar_sum(ph))
        if it < ITERS - 1:
            spread(u3, 0)

    gam = mden[...] / (valid * 0.2)
    soft = ar_sum(0)
    mu = valid * u3
    sub = lax.broadcasted_iota(jnp.int32, (ROWS, 128), 0)
    pick = lax.broadcasted_iota(jnp.int32, (ROWS, 128), 1) == sub + ROWS * (me % 2)

    def own_rows(dense, slot):
        uden[...] = dense
        for v in range(2):
            row = uden[pl.ds(v * 16 + me // 2, 1), :]
            val = jnp.sum(jnp.where(pick, jnp.broadcast_to(row, (ROWS, 128)), 0.0), axis=1, keepdims=True)
            colv[slot, v] = jnp.broadcast_to(val, (ROWS, 128))

    spread(mu * gam, 0)
    spread(gam / soft, 1)

    def unit_of(w):
        return w + par * (UNITS - 1 - 2 * w)

    def unit_ref(q, u):
        return dc_ref.at[pl.ds(pl.multiple_of(q * COLS + u * UNIT, UNIT), UNIT), :]

    def d_copy(q, u, ssem, rsem, dev):
        return remote(unit_ref(q, u), unit_ref(q, u), ssem, rsem, dev)

    def d_core(q, s, u):
        return d_copy(q, u, d_sc.at[s, u], dcore_recv.at[q // 2, u], core)

    def d_wait(q, s, u):
        d_copy(q, u, d_sf.at[0], d_recv.at[s, u], me).wait_recv()

    def own_block(b):
        blk = b + par * (COLS // 128 - 1 - 2 * b)
        k0 = pl.multiple_of(blk * 128, 128)

        def body(i, acc):
            n0 = pl.multiple_of(i * 256, 256)
            e1 = e_ref[0, pl.ds(k0, 128), pl.ds(n0, 256)].reshape(16, 8, 256)
            e2 = e_ref[1, pl.ds(k0, 128), pl.ds(n0, 256)].reshape(16, 8, 256)
            va = jnp.concatenate([vbc[0, pl.ds(k0, 128), :]] * 2, axis=1).reshape(16, 8, 256)
            vb = jnp.concatenate([vbc[1, pl.ds(k0, 128), :]] * 2, axis=1).reshape(16, 8, 256)
            g1 = e1 * ub[1, 0, :, pl.ds(n0, 256)][None] - (e2 * e2 * vb) * ub[0, 1, :, pl.ds(n0, 256)][None]
            g2 = e2 * ub[1, 1, :, pl.ds(n0, 256)][None] - (e1 * e1 * va) * ub[0, 0, :, pl.ds(n0, 256)][None]
            z1 = zc[pl.ds(i * 4, 4), 0:ROWS, :].reshape(256, DIM)
            z2 = zc[pl.ds(i * 4, 4), ROWS:2 * ROWS, :].reshape(256, DIM)
            acc = acc + jnp.dot(g1.reshape(128, 256).astype(BF16), z1, preferred_element_type=F32)
            return acc + jnp.dot(g2.reshape(128, 256).astype(BF16), z2, preferred_element_type=F32)

        acc = lax.fori_loop(0, SAMPLES // 256, body, jnp.zeros((128, DIM), F32))
        dc_ref[pl.ds(pl.multiple_of(j * COLS + blk * 128, 128), 128), :] = acc

    def direct(w):
        u = unit_of(w)
        d_copy(j, u, d_sf.at[u], d_recv.at[0, u], first).start()
        d_copy(j, u, d_ss.at[u], d_recv.at[1, u], second).start()
        d_core(j, 0, u).start()

    def only_core(w):
        d_core(j, 0, unit_of(w)).start()

    @pl.loop(0, DIRECT // 2)
    def _(b):
        own_block(b)
        direct(2 * b)
        direct(2 * b + 1)

    own_block(DIRECT // 2)
    direct(DIRECT - 1)
    only_core(DIRECT)

    @pl.loop(DIRECT // 2 + 1, UNITS // 2)
    def _(b):
        own_block(b)
        only_core(2 * b)
        only_core(2 * b + 1)

    own_rows(mu, 0)
    own_rows(gam, 1)
    own_rows(soft, 2)
    for t in range(1, PLANE):
        o = (j + t) % PLANE
        remote(vall.at[o], vall.at[o], v_send.at[0], v_recv.at[o], me).wait_recv()

    mu1, mu2 = colv[0, 0][:, 0:1], colv[0, 1][:, 0:1]
    gm = colv[1, 0][:, 0:1]
    p1, p2 = colv[2, 0][:, 0:1], colv[2, 1][:, 0:1]
    ip1, ip2 = 1.0 / p1, 1.0 / p2
    lp1, lp2 = jnp.log(p1), jnp.log(p2)
    zown = zc[me, 0:2 * ROWS, :]

    def row_body(i, carry):
        dz, lacc = carry
        k0 = pl.multiple_of(i * 256, 256)
        l0 = pl.multiple_of((i % 4) * 256, 256)
        cb = call[pl.ds(k0, 256), :]
        s = lax.dot_general(zown, cb, NT, preferred_element_type=F32) * INV_T
        e = jnp.exp(s)
        e1, e2 = e[0:ROWS], e[ROWS:]
        q1 = (e1 * e1) * mu1 * vall[i // 4, 0:1, pl.ds(l0, 256)]
        q2 = (e2 * e2) * mu2 * vall[i // 4, 1:2, pl.ds(l0, 256)]
        q1_ref[:, pl.ds(k0, 256)] = q1
        q2_ref[:, pl.ds(k0, 256)] = q2
        lsum = q2 * (s[0:ROWS] - lp1) + q1 * (s[ROWS:] - lp2)
        lacc = lacc + jnp.sum(lsum.reshape(ROWS // 8, 8, 256), axis=0)
        g = jnp.concatenate([(e1 * ip1 - q2) * gm, (e2 * ip2 - q1) * gm], axis=0).astype(BF16)
        return dz + jnp.dot(g, cb, preferred_element_type=F32), lacc

    dz, lacc = lax.fori_loop(0, PROTOS // 256, row_body, (jnp.zeros((2 * ROWS, DIM), F32), jnp.zeros((8, 256), F32)))
    dz1_ref[...] = dz[0:ROWS]
    dz2_ref[...] = dz[ROWS:]
    lpart = jnp.sum(jnp.sum(lacc, axis=0, keepdims=True), axis=1, keepdims=True)
    lbuf[j] = jnp.broadcast_to(lpart, (8, 128))
    l_copies = [remote(lbuf.at[j], lbuf.at[j], l_send.at[t - 1], l_recv.at[j],
                       z * PLANE + (j + t) % PLANE) for t in range(1, PLANE)]
    for cp in l_copies:
        cp.start()

    LAG = 3

    def take_d(w, fwd):
        u = unit_of(w)
        d_wait(jd, 2, u)
        if fwd:
            d_copy(jd, u, d_sz.at[2, u], d_recv.at[2, u], zpart).start()
        d_core(jd, 3, u).start()

    for w in range(DIRECT + LAG):
        if w < DIRECT:
            u = unit_of(w)
            d_wait(jf, 0, u)
            d_copy(jf, u, d_fs.at[u], d_recv.at[2, u], second).start()
            if w < UNITS - DIRECT:
                d_copy(jf, u, d_sz.at[0, u], d_recv.at[0, u], zpart).start()
            d_core(jf, 1, u).start()
            d_wait(js, 1, u)
            if w < UNITS - DIRECT:
                d_copy(js, u, d_sz.at[1, u], d_recv.at[1, u], zpart).start()
            d_core(js, 2, u).start()
        if w >= LAG:
            take_d(w - LAG, w - LAG < UNITS - DIRECT)

    for t in range(1, PLANE):
        o = (j + t) % PLANE
        remote(lbuf.at[o], lbuf.at[o], l_send.at[0], l_recv.at[o], me).wait_recv()
    lsum = lbuf[0]
    for o in range(1, PLANE):
        lsum = lsum + lbuf[o]
    lzbuf[z] = lsum
    lz_copies = [remote(lzbuf.at[z], lzbuf.at[z], lz_send.at[t - 1], lz_recv.at[z],
                        ((z + t) % 4) * PLANE + j) for t in range(1, 4)]
    for cp in lz_copies:
        cp.start()

    for w in range(DIRECT, UNITS):
        u = unit_of(w)
        for s, q in ((0, jf), (1, js), (2, jd)):
            d_wait(q, s, u)
            d_core(q, s + 1, u).start()

    for t in range(1, 4):
        o = (z + t) % 4
        remote(lzbuf.at[o], lzbuf.at[o], lz_send.at[0], lz_recv.at[o], me).wait_recv()
    loss_ref[...] = -(((lzbuf[0] + lzbuf[1]) + lzbuf[2]) + lzbuf[3]) / (2.0 * valid)

    @pl.loop(0, UNITS)
    def _(u):
        for q in range(4):
            d_copy(2 * q + 1 - c, u, d_sf.at[0], dcore_recv.at[q, u], me).wait_recv()

    for cp in pending + v_copies + l_copies + lz_copies:
        cp.wait_send()
    for ph in range(ITERS + 1):
        for cp in ar_copies(ph):
            cp.wait_send()
    for w in range(UNITS):
        u = unit_of(w)
        for s in range(4):
            d_copy(j, u, d_sc.at[s, u], dcore_recv.at[0, u], core).wait_send()
        if w < DIRECT:
            d_copy(j, u, d_sf.at[u], d_recv.at[0, u], first).wait_send()
            d_copy(j, u, d_ss.at[u], d_recv.at[1, u], second).wait_send()
            d_copy(jf, u, d_fs.at[u], d_recv.at[2, u], second).wait_send()
        if w < UNITS - DIRECT:
            for s in range(3):
                d_copy(j, u, d_sz.at[s, u], d_recv.at[s, u], zpart).wait_send()


def solution(mesh):
    def local_step(view_one, view_two, protos, valid_mask):
        m = valid_mask.astype(BF16)
        mk = jnp.broadcast_to(jnp.tile(m, 4)[None], (16, DIM))
        dma = pltpu.SemaphoreType.DMA
        outs = pl.pallas_call(
            kernel,
            out_shape=[
                pltpu.VMEM((ROWS, PROTOS), F32),
                pltpu.VMEM((ROWS, PROTOS), F32),
                pltpu.VMEM((8, 128), F32),
                pltpu.VMEM((ROWS, DIM), F32),
                pltpu.VMEM((ROWS, DIM), F32),
                pltpu.VMEM((PROTOS, DIM), F32),
            ],
            in_specs=[pl.BlockSpec(memory_space=pl.ANY)] * 4,
            out_specs=[pl.BlockSpec(memory_space=pltpu.VMEM)] * 6,
            scratch_shapes=[
                pltpu.VMEM((DEVS, SLAB, DIM), BF16),
                pltpu.VMEM((PROTOS, DIM), BF16),
                pltpu.VMEM((2, COLS, SAMPLES), F32),
                pltpu.VMEM((2, COLS, 128), F32),
                pltpu.VMEM((32, 128), F32),
                pltpu.VMEM((32, 128), F32),
                pltpu.VMEM((2, 2, 8, SAMPLES), F32),
                pltpu.VMEM((ITERS + 1, PLANE, 32, 128), F32),
                pltpu.VMEM((PLANE, 2, COLS), F32),
                pltpu.VMEM((PLANE, 8, 128), F32),
                pltpu.VMEM((4, 8, 128), F32),
                pltpu.VMEM((3, 2, ROWS, 128), F32),
                dma((4,)), dma((31,)), dma((DEVS,)),
                dma((ITERS + 1, PLANE - 1)), dma((ITERS + 1, PLANE)),
                dma((PLANE - 1,)), dma((PLANE,)),
                dma((PLANE - 1,)), dma((PLANE,)), dma((3,)), dma((4,)),
                dma((3, UNITS)), dma((4, UNITS)), dma((UNITS,)), dma((UNITS,)), dma((4, UNITS)),
                dma((UNITS,)), dma((3, UNITS)),
            ],
            compiler_params=pltpu.CompilerParams(
                collective_id=0, has_side_effects=True, vmem_limit_bytes=44 << 20),
        )(view_one, view_two, mk, protos)
        q1, q2, loss, dz1, dz2, dc = outs
        return q1, q2, loss[0, 0], dz1, dz2, dc

    return jax.shard_map(
        local_step,
        mesh=mesh,
        in_specs=(P("data", None), P("data", None), P(None, None), P("data")),
        out_specs=(P("data", None), P("data", None), P(), P("data", None), P("data", None), P(None, None)),
        check_vma=False,
    )
```

time: 535 us -> 135 us (0.25)
  waiting for transfers between devices: 255 us -> 0 us
  blocking collectives: 204 us -> 0 us
  Pallas kernels: 0 us -> 125 us
  other arithmetic: 30.8 us -> 0.66 us
  matrix products: 18.2 us -> 0 us
  between operations: 18.7 us -> 0.64 us
    psum x2 -> x0, waiting for transfers between devices: 255 us -> none  [the longest x1 128 us: value_a14(): col_sum = lax.psum(jnp.sum(transport, axis=0, keepdims=True), 'data')]
    psum x5 -> x0, blocking collectives: 204 us -> none  [the longest x3 120 us: value_a14(): col_sum = lax.psum(jnp.sum(transport, axis=0, keepdims=True), 'data')]
    pallas_call x0 -> x1, Pallas kernels: none -> 125 us  [local_step(): pl.pallas_call(kernel, out_shape=[pltpu.VMEM((ROWS, PROTOS), F32), pltpu....]
    reduce_sum x12 -> x0, other arithmetic: 18.4 us -> none  [the longest x4 6.74 us: value_a14(): row_sum = jnp.sum(transport, axis=1, keepdims=True) + (1.0 - weights)]
    dot_general x6 -> x0, matrix products: 18.2 us -> none  [the longest x1 5.16 us: local_step(): jnp.einsum('nd,kd->nk', view_two, protos, preferred_element_type=jnp.floa...]
    convert_element_type x3 -> x1, other arithmetic: 7.31 us -> 0.66 us  [local_step(): m = valid_mask.astype(BF16)]
  transfers between devices with their start and end apart: 2 -> 0, of which waited for: 2 -> 0; matrix products, arithmetic and copies ran while one was open for 2% -> 0% of each run, Pallas kernels for 0% -> 0%
where the time goes in v1:
time: 135 us; the launch traced here: 134 us
  Pallas kernels  125 us (93%)
  local copies, waits for them, and re-layouts  8.5 us (6%)
    pallas_call x1, Pallas kernels, local_step(): pl.pallas_call(kernel, out_shape=[pltpu.VMEM((ROWS, PROTOS), F32), pltpu....  125 us
    unnamed x5, local copies, waits for them, and re-layouts  7.29 us

profile of v1, /device:TPU:0, one launch (start us, length us, event | category | flops | bytes accessed | tf_op | source)
XLA Modules:
  0.0 134.4 jit_solution(10543890462722790557)
XLA Ops:
  0.6 0.7 convert_element_type.3
  1.3 0.1 broadcast_in_dim.7
  1.4 0.6 broadcast_in_dim.8.mk_hbm
  2.0 124.6 %shard_map.91 = (f32[64,8192]{1,0:T(8,128)S(1)}, f32[64,8192]{1,0:T(8,128)S(1)}, f32[8,128]{1,0:T(8,128)S(1)}, f32[64,256]{1,0:T(8,128)S(1)}, f32[64,256]{1,0:T(8,128)S(1)}, /*index=5*/f32[8192,256]{1,0:T(8,128)S(1)}) custom-call(bf16[64,256]{1,0:T(8,128)(2,1)} %v1_hbm.1, bf16[64,256]{1,0:T(8,128)(2,1)} %v2_hbm.1, bf16[16,256]{1,0:T(8,128)(2,1)} %broadcast_in_dim.8.mk_hbm, ...), custom_call_target="tpu_custom_call" | custom-call | tf_op jit(solution)/shard_map/pallas_call | solution.py:430
  126.6 0.5 slice.3
  127.1 1.3 copy.15
  128.4 0.6 copy.17
  129.0 0.6 copy.18
  129.7 1.3 copy.16
  131.0 3.4 %copy.19 = f32[8192,256]{1,0:T(8,128)} copy(f32[8192,256]{1,0:T(8,128)S(1)} %get-tuple-element.23) | data formatting | bytes 16777216
  (1 shorter events, 0.0 us)

commit v2 on v1

--- a/solution.py
+++ b/solution.py
@@ -13,22 +13,24 @@
 DEVS = 32
 PLANE = 8
 SAMPLES = ROWS * DEVS
+MB = 256
 PROTOS = 8192
 DIM = 256
 COLS = PROTOS // PLANE
 ITERS = 3
 INV_T = 10.0
-SLAB = 2 * ROWS + 16
+SLAB = 2 * ROWS
 UNIT = 64
 UNITS = COLS // UNIT
 DIRECT = 11
+LOG2E = 1.4426950408889634
 NT = (((1,), (1,)), ((), ()))
 
 
 def kernel(v1_hbm, v2_hbm, mk_hbm, c_hbm,
            q1_ref, q2_ref, loss_ref, dz1_ref, dz2_ref, dc_ref,
-           zc, call, e_ref, vbc, mden, uden, ub, rbuf, vall, lbuf, lzbuf, colv,
-           lsem, z_send, z_recv, ar_send, ar_recv, v_send, v_recv,
+           zc, mi, mbuf, call, e_ref, a_ref, vbc, mden, uden, ub, rbuf, vall, lbuf, lzbuf, colv,
+           lsem, z_send, z_recv, m_send, m_recv, ar_send, ar_recv, v_send, v_recv,
            l_send, l_recv, lz_send, lz_recv,
            d_recv, dcore_recv, d_sf, d_ss, d_sc, d_fs, d_sz):
     me = lax.axis_index("data")
@@ -57,7 +59,7 @@
     own = [
         pltpu.make_async_copy(v1_hbm, zc.at[me, pl.ds(0, ROWS), :], lsem.at[0]),
         pltpu.make_async_copy(v2_hbm, zc.at[me, pl.ds(ROWS, ROWS), :], lsem.at[1]),
-        pltpu.make_async_copy(mk_hbm, zc.at[me, pl.ds(2 * ROWS, 16), :], lsem.at[2]),
+        pltpu.make_async_copy(mk_hbm, mi, lsem.at[2]),
     ]
     for cp in own:
         cp.start()
@@ -65,6 +67,8 @@
     c_copy.start()
     for cp in own:
         cp.wait()
+    mrow = mi[...].astype(F32)
+    mbuf[me] = jnp.concatenate([mrow, mrow], axis=1)
     pl.semaphore_wait(barrier, PLANE - 1 + 3)
 
     def remote(src, dst, ssem, rsem, dev):
@@ -74,12 +78,15 @@
     pending = []
 
     def z_copy(i, dev):
-        cp = remote(zc.at[i], zc.at[i], z_send.at[len(pending)], z_recv.at[i], dev)
-        pending.append(cp)
-        cp.start()
+        k = len(pending) // 2
+        for cp in (remote(zc.at[i], zc.at[i], z_send.at[k], z_recv.at[i], dev),
+                   remote(mbuf.at[i], mbuf.at[i], m_send.at[k], m_recv.at[i], dev)):
+            pending.append(cp)
+            cp.start()
 
     def z_wait(i):
         remote(zc.at[i], zc.at[i], z_send.at[0], z_recv.at[i], me).wait_recv()
+        remote(mbuf.at[i], mbuf.at[i], m_send.at[0], m_recv.at[i], me).wait_recv()
 
     def rel(t):
         return ((z + t) % 4) * PLANE
@@ -105,45 +112,53 @@
         for q in range(4):
             z_wait(rel(t) + 2 * q + 1 - c)
 
+    def scores(t, v):
+        p = (z + t) % 4
+
+        def body(h, carry):
+            zb = zc[pl.ds(p * PLANE + h * 4, 4), v * ROWS:(v + 1) * ROWS, :].reshape(4 * ROWS, DIM)
+            n0 = pl.multiple_of(p * 512 + h * 256, 256)
+            acc = jnp.zeros((8, 256), F32)
+            for kb in range(COLS // MB):
+                cs = call[pl.ds(pl.multiple_of(j * COLS + kb * MB, MB), MB), :]
+                s = lax.dot_general(cs, zb, NT, preferred_element_type=F32)
+                e = jnp.exp2(s * (INV_T * LOG2E))
+                e_ref[v, kb * MB:(kb + 1) * MB, pl.ds(n0, 256)] = e
+                a_ref[v, kb * MB:(kb + 1) * MB, pl.ds(n0, 256)] = e * e
+                acc = acc + jnp.sum(e.reshape(MB // 8, 8, 256), axis=0)
+            tot = jnp.sum(acc, axis=0, keepdims=True)
+            for b in range(2):
+                rbuf[0, j, pl.ds(v * 16 + p * 4 + h * 2 + b, 1), :] = tot[:, b * 128:(b + 1) * 128]
+            return carry
+
+        lax.fori_loop(0, 2, body, 0)
+
     take_f(0)
+    take_s(0)
     for t in range(1, 4):
         z_wait(rel(t) + j)
         z_copy(rel(t) + j, first)
         z_copy(rel(t) + j, second)
         z_copy(rel(t) + j, core)
-    take_s(0)
-    for t in range(1, 4):
-        take_f(t)
+    c_copy.wait()
+    take_core(0)
+    scores(0, 0)
+    take_f(1)
+    scores(0, 1)
+    take_f(2)
+    take_f(3)
     take_s(1)
-    c_copy.wait()
-
-    def scores(t):
-        p = (z + t) % 4
-        for v in range(2):
-            zb = zc[pl.ds(p * PLANE, PLANE), v * ROWS:(v + 1) * ROWS, :].reshape(PLANE * ROWS, DIM)
-
-            def body(kb, acc, v=v, zb=zb):
-                cs = call[pl.ds(pl.multiple_of(j * COLS + kb * 128, 128), 128), :]
-                s = lax.dot_general(cs, zb, NT, preferred_element_type=F32)
-                e = jnp.exp(s * INV_T)
-                e_ref[v, pl.ds(pl.multiple_of(kb * 128, 128), 128), pl.ds(pl.multiple_of(p * 512, 512), 512)] = e
-                return acc + jnp.sum(e.reshape(16, 8, 512), axis=0)
-
-            acc = lax.fori_loop(0, COLS // 128, body, jnp.zeros((8, 512), F32))
-            tot = jnp.sum(acc, axis=0, keepdims=True)
-            for b in range(4):
-                rbuf[0, j, pl.ds(v * 16 + p * 4 + b, 1), :] = tot[:, b * 128:(b + 1) * 128]
-
-    take_core(0)
-    scores(0)
+    take_core(1)
+    scores(1, 0)
     take_s(2)
-    take_core(1)
-    scores(1)
+    scores(1, 1)
     take_s(3)
     take_core(2)
-    scores(2)
+    scores(2, 0)
+    scores(2, 1)
     take_core(3)
-    scores(3)
+    scores(3, 0)
+    scores(3, 1)
 
     def ar_copies(ph):
         return [remote(rbuf.at[ph, j], rbuf.at[ph, j], ar_send.at[ph, t - 1], ar_recv.at[ph, j],
@@ -165,9 +180,7 @@
 
     lane = lax.broadcasted_iota(jnp.int32, (1, 128), 1)
     for b in range(16):
-        even = zc[2 * b, 2 * ROWS:2 * ROWS + 16, 0:128].astype(F32)[0:1]
-        odd = zc[2 * b + 1, 2 * ROWS:2 * ROWS + 16, 0:128].astype(F32)[0:1]
-        mrow = jnp.where(lane < ROWS, even, odd)
+        mrow = jnp.where(lane < ROWS, mbuf[2 * b], mbuf[2 * b + 1])
         mden[pl.ds(b, 1), :] = mrow
         mden[pl.ds(16 + b, 1), :] = mrow
     valid = jnp.sum(jnp.sum(mden[0:16, :], axis=0, keepdims=True), axis=1, keepdims=True)
@@ -180,36 +193,54 @@
 
     spread(mden[...], 0)
 
-    KB = 32
+    GRP = 4
+    LB = SAMPLES // 128
 
     def sweep(ph):
         for v in range(2):
-            u = ub[0, v]
-
-            def rows(kb):
-                w = e_ref[v, pl.ds(pl.multiple_of(kb * KB, KB), KB), :]
-                return (w * w).reshape(KB // 8, 8, SAMPLES)
-
-            def body(kb, carry):
-                acc, vprev = carry
-                wu = rows(kb) * u[None]
-                part = wu[:, :, 0:128]
-                for b in range(1, 16):
-                    part = part + wu[:, :, b * 128:(b + 1) * 128]
-                col = jnp.sum(part.reshape(KB, 128), axis=1, keepdims=True)
-                vnew = jnp.broadcast_to(1.0 / (PROTOS * col), (KB, 128))
-                vbc[v, pl.ds(pl.multiple_of(kb * KB, KB), KB), :] = vnew
-                old = rows(jnp.maximum(kb - 1, 0))
-                vb = jnp.concatenate([vprev.reshape(KB // 8, 8, 128)] * 16, axis=2)
-                acc = acc + jnp.sum(old * vb, axis=0)
-                return acc, vnew
-
-            acc, vlast = lax.fori_loop(0, COLS // KB, body, (jnp.zeros((8, SAMPLES), F32), jnp.zeros((KB, 128), F32)))
-            vb = jnp.concatenate([vlast.reshape(KB // 8, 8, 128)] * 16, axis=2)
-            acc = acc + jnp.sum(rows(COLS // KB - 1) * vb, axis=0)
-            tot = jnp.sum(acc, axis=0, keepdims=True)
-            for b in range(16):
-                rbuf[ph, j, pl.ds(v * 16 + b, 1), :] = tot[:, b * 128:(b + 1) * 128]
+            u = [ub[0, v, :, b * 128:(b + 1) * 128] for b in range(LB)]
+
+            def tile(row, b):
+                return a_ref[v, pl.ds(row, 8), b * 128:(b + 1) * 128]
+
+            def add_rows(i, acc, vs):
+                for g in range(GRP):
+                    row = pl.multiple_of((i * GRP + g) * 8, 8)
+                    for b in range(LB):
+                        acc[b] = acc[b] + tile(row, b) * vs[g]
+                return acc
+
+            def body(i, carry):
+                acc, vprev = list(carry[:LB]), list(carry[LB:])
+                vnew = []
+                for g in range(GRP):
+                    row = pl.multiple_of((i * GRP + g) * 8, 8)
+                    parts = [tile(row, b) * u[b] for b in range(2)]
+                    for b in range(2, LB):
+                        parts[b % 2] = parts[b % 2] + tile(row, b) * u[b]
+                    col = jnp.sum(parts[0] + parts[1], axis=1, keepdims=True)
+                    vg = jnp.broadcast_to(1.0 / (PROTOS * col), (8, 128))
+                    vbc[v, pl.ds(row, 8), :] = vg
+                    vnew.append(vg)
+                acc = add_rows(jnp.maximum(i - 1, 0), acc, vprev)
+                return tuple(acc) + tuple(vnew)
+
+            zero = jnp.zeros((8, 128), F32)
+            steps = COLS // (8 * GRP)
+            out = lax.fori_loop(0, steps, body, (zero,) * (LB + GRP))
+            acc = add_rows(steps - 1, list(out[:LB]), out[LB:])
+            for b in range(LB):
+                rbuf[ph, j, pl.ds(v * 16 + b, 1), :] = jnp.sum(acc[b], axis=0, keepdims=True)
+
+    def row_scores(lo, hi):
+        def body(i, carry):
+            k0 = pl.multiple_of(i * 256, 256)
+            rs = lax.dot_general(zc[me], call[pl.ds(k0, 256), :], NT, preferred_element_type=F32)
+            q1_ref[:, pl.ds(k0, 256)] = rs[0:ROWS]
+            q2_ref[:, pl.ds(k0, 256)] = rs[ROWS:]
+            return carry
+
+        lax.fori_loop(lo, hi, body, 0)
 
     v_copies = []
     u3 = None
@@ -230,6 +261,7 @@
                                z * PLANE + (j + t) % PLANE) for t in range(1, PLANE)]
             for cp in v_copies:
                 cp.start()
+        row_scores((0, 11, 22)[it], (11, 22, 32)[it])
         ar_wait(ph)
         u3 = mden[...] / (valid * ar_sum(ph))
         if it < ITERS - 1:
@@ -286,30 +318,56 @@
         acc = lax.fori_loop(0, SAMPLES // 256, body, jnp.zeros((128, DIM), F32))
         dc_ref[pl.ds(pl.multiple_of(j * COLS + blk * 128, 128), 128), :] = acc
 
-    def direct(w):
-        u = unit_of(w)
-        d_copy(j, u, d_sf.at[u], d_recv.at[0, u], first).start()
+    def send_own(w):
+        u = unit_of(w)
+        if w < DIRECT:
+            d_copy(j, u, d_sf.at[u], d_recv.at[0, u], first).start()
+        d_core(j, 0, u).start()
+
+    def send_second(w):
+        u = unit_of(w)
         d_copy(j, u, d_ss.at[u], d_recv.at[1, u], second).start()
-        d_core(j, 0, u).start()
-
-    def only_core(w):
-        d_core(j, 0, unit_of(w)).start()
-
-    @pl.loop(0, DIRECT // 2)
-    def _(b):
+
+    def take_first(w):
+        u = unit_of(w)
+        d_wait(jf, 0, u)
+        d_copy(jf, u, d_fs.at[u], d_recv.at[2, u], second).start()
+        if w < UNITS - DIRECT:
+            d_copy(jf, u, d_sz.at[0, u], d_recv.at[0, u], zpart).start()
+        d_core(jf, 1, u).start()
+
+    def take_second(w):
+        u = unit_of(w)
+        d_wait(js, 1, u)
+        if w < UNITS - DIRECT:
+            d_copy(js, u, d_sz.at[1, u], d_recv.at[1, u], zpart).start()
+        d_core(js, 2, u).start()
+
+    def take_diag(w):
+        u = unit_of(w)
+        d_wait(jd, 2, u)
+        if w < UNITS - DIRECT:
+            d_copy(jd, u, d_sz.at[2, u], d_recv.at[2, u], zpart).start()
+        d_core(jd, 3, u).start()
+
+    def step(w):
+        take_first(w)
+        if w + 3 < DIRECT:
+            send_second(w + 3)
+        take_second(w)
+        if w >= 3:
+            take_diag(w - 3)
+
+    for b in range(UNITS // 2):
         own_block(b)
-        direct(2 * b)
-        direct(2 * b + 1)
-
-    own_block(DIRECT // 2)
-    direct(DIRECT - 1)
-    only_core(DIRECT)
-
-    @pl.loop(DIRECT // 2 + 1, UNITS // 2)
-    def _(b):
-        own_block(b)
-        only_core(2 * b)
-        only_core(2 * b + 1)
+        send_own(2 * b)
+        send_own(2 * b + 1)
+        if b < 2:
+            send_second(2 * b)
+        if b == 0:
+            send_second(1)
+        if b >= 2:
+            step(b - 2)
 
     own_rows(mu, 0)
     own_rows(gam, 1)
@@ -323,26 +381,31 @@
     p1, p2 = colv[2, 0][:, 0:1], colv[2, 1][:, 0:1]
     ip1, ip2 = 1.0 / p1, 1.0 / p2
     lp1, lp2 = jnp.log(p1), jnp.log(p2)
-    zown = zc[me, 0:2 * ROWS, :]
 
     def row_body(i, carry):
         dz, lacc = carry
         k0 = pl.multiple_of(i * 256, 256)
         l0 = pl.multiple_of((i % 4) * 256, 256)
         cb = call[pl.ds(k0, 256), :]
-        s = lax.dot_general(zown, cb, NT, preferred_element_type=F32) * INV_T
-        e = jnp.exp(s)
-        e1, e2 = e[0:ROWS], e[ROWS:]
+        s1 = q1_ref[:, pl.ds(k0, 256)] * INV_T
+        s2 = q2_ref[:, pl.ds(k0, 256)] * INV_T
+        e1 = jnp.exp2(s1 * LOG2E)
+        e2 = jnp.exp2(s2 * LOG2E)
         q1 = (e1 * e1) * mu1 * vall[i // 4, 0:1, pl.ds(l0, 256)]
         q2 = (e2 * e2) * mu2 * vall[i // 4, 1:2, pl.ds(l0, 256)]
         q1_ref[:, pl.ds(k0, 256)] = q1
         q2_ref[:, pl.ds(k0, 256)] = q2
-        lsum = q2 * (s[0:ROWS] - lp1) + q1 * (s[ROWS:] - lp2)
+        lsum = q2 * (s1 - lp1) + q1 * (s2 - lp2)
         lacc = lacc + jnp.sum(lsum.reshape(ROWS // 8, 8, 256), axis=0)
         g = jnp.concatenate([(e1 * ip1 - q2) * gm, (e2 * ip2 - q1) * gm], axis=0).astype(BF16)
         return dz + jnp.dot(g, cb, preferred_element_type=F32), lacc
 
-    dz, lacc = lax.fori_loop(0, PROTOS // 256, row_body, (jnp.zeros((2 * ROWS, DIM), F32), jnp.zeros((8, 256), F32)))
+    carry = (jnp.zeros((2 * ROWS, DIM), F32), jnp.zeros((8, 256), F32))
+    cuts = (0, 7, 14, 20, 26, 32)
+    for i in range(5):
+        carry = lax.fori_loop(cuts[i], cuts[i + 1], row_body, carry)
+        step(UNITS // 2 - 2 + i)
+    dz, lacc = carry
     dz1_ref[...] = dz[0:ROWS]
     dz2_ref[...] = dz[ROWS:]
     lpart = jnp.sum(jnp.sum(lacc, axis=0, keepdims=True), axis=1, keepdims=True)
@@ -352,29 +415,8 @@
     for cp in l_copies:
         cp.start()
 
-    LAG = 3
-
-    def take_d(w, fwd):
-        u = unit_of(w)
-        d_wait(jd, 2, u)
-        if fwd:
-            d_copy(jd, u, d_sz.at[2, u], d_recv.at[2, u], zpart).start()
-        d_core(jd, 3, u).start()
-
-    for w in range(DIRECT + LAG):
-        if w < DIRECT:
-            u = unit_of(w)
-            d_wait(jf, 0, u)
-            d_copy(jf, u, d_fs.at[u], d_recv.at[2, u], second).start()
-            if w < UNITS - DIRECT:
-                d_copy(jf, u, d_sz.at[0, u], d_recv.at[0, u], zpart).start()
-            d_core(jf, 1, u).start()
-            d_wait(js, 1, u)
-            if w < UNITS - DIRECT:
-                d_copy(js, u, d_sz.at[1, u], d_recv.at[1, u], zpart).start()
-            d_core(js, 2, u).start()
-        if w >= LAG:
-            take_d(w - LAG, w - LAG < UNITS - DIRECT)
+    for w in range(DIRECT - 3, DIRECT):
+        take_diag(w)
 
     for t in range(1, PLANE):
         o = (j + t) % PLANE
@@ -388,7 +430,7 @@
     for cp in lz_copies:
         cp.start()
 
-    for w in range(DIRECT, UNITS):
+    for w in reversed(range(DIRECT, UNITS)):
         u = unit_of(w)
         for s, q in ((0, jf), (1, js), (2, jd)):
             d_wait(q, s, u)
@@ -397,7 +439,8 @@
     for t in range(1, 4):
         o = (z + t) % 4
         remote(lzbuf.at[o], lzbuf.at[o], lz_send.at[0], lz_recv.at[o], me).wait_recv()
-    loss_ref[...] = -(((lzbuf[0] + lzbuf[1]) + lzbuf[2]) + lzbuf[3]) / (2.0 * valid)
+    loss = -(((lzbuf[0] + lzbuf[1]) + lzbuf[2]) + lzbuf[3]) / (2.0 * valid)
+    loss_ref[...] = loss[0:1, 0:1]
 
     @pl.loop(0, UNITS)
     def _(u):
@@ -422,17 +465,24 @@
                 d_copy(j, u, d_sz.at[s, u], d_recv.at[s, u], zpart).wait_send()
 
 
+def store_kernel(*refs):
+    srcs, dsts, sem = refs[:6], refs[6:12], refs[12]
+    copies = [pltpu.make_async_copy(s, d, sem.at[i]) for i, (s, d) in enumerate(zip(srcs, dsts))]
+    for cp in copies:
+        cp.start()
+    for cp in copies:
+        cp.wait()
+
+
 def solution(mesh):
     def local_step(view_one, view_two, protos, valid_mask):
-        m = valid_mask.astype(BF16)
-        mk = jnp.broadcast_to(jnp.tile(m, 4)[None], (16, DIM))
         dma = pltpu.SemaphoreType.DMA
         outs = pl.pallas_call(
             kernel,
             out_shape=[
                 pltpu.VMEM((ROWS, PROTOS), F32),
                 pltpu.VMEM((ROWS, PROTOS), F32),
-                pltpu.VMEM((8, 128), F32),
+                pltpu.VMEM((1, 1), F32),
                 pltpu.VMEM((ROWS, DIM), F32),
                 pltpu.VMEM((ROWS, DIM), F32),
                 pltpu.VMEM((PROTOS, DIM), F32),
@@ -441,7 +491,10 @@
             out_specs=[pl.BlockSpec(memory_space=pltpu.VMEM)] * 6,
             scratch_shapes=[
                 pltpu.VMEM((DEVS, SLAB, DIM), BF16),
+                pltpu.VMEM((1, ROWS), jnp.int32),
+                pltpu.VMEM((DEVS, 1, 128), F32),
                 pltpu.VMEM((PROTOS, DIM), BF16),
+                pltpu.VMEM((2, COLS, SAMPLES), F32),
                 pltpu.VMEM((2, COLS, SAMPLES), F32),
                 pltpu.VMEM((2, COLS, 128), F32),
                 pltpu.VMEM((32, 128), F32),
@@ -452,7 +505,7 @@
                 pltpu.VMEM((PLANE, 8, 128), F32),
                 pltpu.VMEM((4, 8, 128), F32),
                 pltpu.VMEM((3, 2, ROWS, 128), F32),
-                dma((4,)), dma((31,)), dma((DEVS,)),
+                dma((4,)), dma((31,)), dma((DEVS,)), dma((31,)), dma((DEVS,)),
                 dma((ITERS + 1, PLANE - 1)), dma((ITERS + 1, PLANE)),
                 dma((PLANE - 1,)), dma((PLANE,)),
                 dma((PLANE - 1,)), dma((PLANE,)), dma((3,)), dma((4,)),
@@ -460,10 +513,18 @@
                 dma((UNITS,)), dma((3, UNITS)),
             ],
             compiler_params=pltpu.CompilerParams(
-                collective_id=0, has_side_effects=True, vmem_limit_bytes=44 << 20),
-        )(view_one, view_two, mk, protos)
+                collective_id=0, has_side_effects=True, vmem_limit_bytes=48 << 20),
+        )(view_one, view_two, valid_mask.reshape(1, ROWS), protos)
+        outs = pl.pallas_call(
+            store_kernel,
+            out_shape=[jax.ShapeDtypeStruct(o.shape, o.dtype) for o in outs],
+            in_specs=[pl.BlockSpec(memory_space=pltpu.VMEM)] * 6,
+            out_specs=[pl.BlockSpec(memory_space=pl.ANY)] * 6,
+            scratch_shapes=[dma((6,))],
+            compiler_params=pltpu.CompilerParams(vmem_limit_bytes=4 << 20),
+        )(*[pltpu.with_memory_space_constraint(o, pltpu.VMEM) for o in outs])
         q1, q2, loss, dz1, dz2, dc = outs
-        return q1, q2, loss[0, 0], dz1, dz2, dc
+        return q1, q2, loss.reshape(()), dz1, dz2, dc
 
     return jax.shard_map(
         local_step,

time: 135 us -> 104 us (0.77)
  Pallas kernels: 125 us -> 103 us
  local copies, waits for them, and re-layouts: 8.5 us -> 0 us
    pallas_call x1, Pallas kernels: 125 us -> 97.7 us  [local_step(): pl.pallas_call(kernel, out_shape=[pltpu.VMEM((ROWS, PROTOS), F32), pltpu....]
    unnamed x5 -> x0, local copies, waits for them, and re-layouts: 7.29 us -> none
    pallas_call x0 -> x1, Pallas kernels: none -> 5.5 us  [local_step(): pl.pallas_call(store_kernel, out_shape=[jax.ShapeDtypeStruct(o.shape, o.d...]
where the time goes in v2:
time: 104 us
  Pallas kernels  103 us (99%)
    pallas_call x1, Pallas kernels, local_step(): pl.pallas_call(kernel, out_shape=[pltpu.VMEM((ROWS, PROTOS), F32), pltpu....  97.7 us
    pallas_call x1, Pallas kernels, local_step(): pl.pallas_call(store_kernel, out_shape=[jax.ShapeDtypeStruct(o.shape, o.d...  5.5 us

profile of v2, /device:TPU:0, one launch (start us, length us, event | category | flops | bytes accessed | tf_op | source)
XLA Modules:
  0.0 103.8 jit_solution(15687304179803056918)
XLA Ops:
  0.6 97.7 %shard_map.91 = (f32[64,8192]{1,0:T(8,128)S(1)}, f32[64,8192]{1,0:T(8,128)S(1)}, f32[1,1]{1,0:T(1,128)}, f32[64,256]{1,0:T(8,128)S(1)}, f32[64,256]{1,0:T(8,128)S(1)}, /*index=5*/f32[8192,256]{1,0:T(8,128)S(1)}) custom-call(bf16[64,256]{1,0:T(8,128)(2,1)} %v1_hbm.1, bf16[64,256]{1,0:T(8,128)(2,1)} %v2_hbm.1, s32[1,64]{1,0:T(1,128)} %bitcast.2, ...), custom_call_target="tpu_custom_call" | custom-call | tf_op jit(solution)/shard_map/pallas_call | solution.py:480
  98.3 5.5 %shard_map.92 = (f32[64,8192]{1,0:T(8,128)}, f32[64,8192]{1,0:T(8,128)}, f32[1,1]{1,0:T(1,128)}, f32[64,256]{1,0:T(8,128)}, f32[64,256]{1,0:T(8,128)}, /*index=5*/f32[8192,256]{1,0:T(8,128)}) custom-call(f32[64,8192]{1,0:T(8,128)S(1)} %get-tuple-element.18.refs_0_, f32[64,8192]{1,0:T(8,128)S(1)} %get-tuple-element.19.refs_1_, ...), custom_call_target="tpu_custom_call" | custom-call | tf_op jit(solution)/shard_map/pallas_call | solution.py:518

commit v3 on v2

v3 whole, which is shorter than its diff:
```python
import jax
import jax.numpy as jnp
from jax import lax
from jax.experimental import pallas as pl
from jax.experimental.pallas import tpu as pltpu
from jax.sharding import PartitionSpec as P

MESH = pl.DeviceIdType.MESH
F32 = jnp.float32
BF16 = jnp.bfloat16

ROWS = 64
SLAB = 2 * ROWS
DEVS = 32
PLANE = 8
SAMPLES = ROWS * DEVS
MB = 256
PROTOS = 8192
DIM = 256
COLS = PROTOS // PLANE
ITERS = 3
LANES = 128
PLANES = DEVS // PLANE
PEERS = range(1, PLANE)
BLK = 2 * LANES
DENSE = SAMPLES // LANES
INV_T = 10.0
UNIT = 64
UNITS = COLS // UNIT
BLOCKS = COLS // LANES
DIRECT = 11
GRP = 32
LOG2E = 1.4426950408889634
ROW_CUTS = (5, 11, 17, 32)
NT = (((1,), (1,)), ((), ()))


def kernel(v1_hbm, v2_hbm, mk_hbm, c_hbm,
           q1_ref, q2_ref, loss_ref, dz1_ref, dz2_ref, dc_ref,
           zc, mi, mbuf, call, e_ref, a_ref, vbc, mden, uden, ub, rbuf, vall, lbuf, lzbuf,
           lsem, z_send, z_recv, m_send, m_recv, ar_send, ar_recv, v_send, v_recv,
           l_send, l_recv, lz_send, lz_recv,
           d_recv, dcore_recv, d_sf, d_ss, d_sc, d_fs, d_sz):
    me = lax.axis_index("data")
    z = me // PLANE
    j = me % PLANE
    c = j % 2
    x = (j // 2) % 2
    y = j // 4
    jx = j + 2 - 4 * x
    jy = j + 4 - 8 * y
    jd = (6 - 2 * (j // 2)) + c
    jf = jx + c * (jy - jx)
    js = jy + c * (jx - jy)
    core = me + 1 - 2 * c
    first = z * PLANE + jf
    second = z * PLANE + js
    par = z % 2
    planes = (z, z + 1 - 2 * par, z + 2 - PLANES * (z // 2), PLANES - 1 - z)
    zpart = planes[1] * PLANE + j
    peers = [z * PLANE + (j + t) % PLANE for t in PEERS]
    slots = [(j + t) % PLANE for t in PEERS]
    zpeers = [p * PLANE + j for p in planes[1:]]

    barrier = pltpu.get_barrier_semaphore()
    for dev in peers + zpeers:
        pl.semaphore_signal(barrier, inc=1, device_id=(dev,), device_id_type=MESH)

    own = [
        pltpu.make_async_copy(v1_hbm, zc.at[me, pl.ds(0, ROWS), :], lsem.at[0]),
        pltpu.make_async_copy(v2_hbm, zc.at[me, pl.ds(ROWS, ROWS), :], lsem.at[1]),
        pltpu.make_async_copy(mk_hbm, mi, lsem.at[2]),
    ]
    for cp in own:
        cp.start()
    c_copy = pltpu.make_async_copy(c_hbm, call, lsem.at[3])
    c_copy.start()
    for cp in own:
        cp.wait()
    mrow = mi[...].astype(F32)
    mbuf[me] = jnp.concatenate([mrow, mrow], axis=1)
    pl.semaphore_wait(barrier, len(peers + zpeers))

    def remote(src, dst, ssem, rsem, dev):
        return pltpu.make_async_remote_copy(src_ref=src, dst_ref=dst, send_sem=ssem, recv_sem=rsem,
                                            device_id=(dev,), device_id_type=MESH)

    pending = []

    def z_copy(i, dev):
        k = len(pending) // 2
        for cp in (remote(zc.at[i], zc.at[i], z_send.at[k], z_recv.at[i], dev),
                   remote(mbuf.at[i], mbuf.at[i], m_send.at[k], m_recv.at[i], dev)):
            pending.append(cp)
            cp.start()

    def z_wait(i):
        remote(zc.at[i], zc.at[i], z_send.at[0], z_recv.at[i], me).wait_recv()
        remote(mbuf.at[i], mbuf.at[i], m_send.at[0], m_recv.at[i], me).wait_recv()

    def rel(t):
        return planes[t] * PLANE

    def row_scores(lo, hi):
        def body(i, carry):
            k0 = pl.multiple_of(i * BLK, BLK)
            rs = lax.dot_general(zc[me], call[pl.ds(k0, BLK), :], NT, preferred_element_type=F32)
            q1_ref[:, pl.ds(k0, BLK)] = rs[:ROWS]
            q2_ref[:, pl.ds(k0, BLK)] = rs[ROWS:]
            return carry

        lax.fori_loop(lo, hi, body, 0)

    z_copy(me, first)
    z_copy(me, second)
    for dev in zpeers:
        z_copy(me, dev)
    z_copy(me, core)
    c_copy.wait()
    row_scores(0, ROW_CUTS[0])

    def take_z(t):
        z_wait(rel(t) + j)
        z_copy(rel(t) + j, first)
        if t != 1:
            z_copy(rel(t) + j, second)
        z_copy(rel(t) + j, core)

    def take_f(t):
        z_wait(rel(t) + jf)
        if t != 1:
            z_copy(rel(t) + jf, second)
        z_copy(rel(t) + jf, core)

    def take_s(t):
        z_wait(rel(t) + js)
        if t == 0:
            z_copy(rel(t) + js, zpart)
        z_copy(rel(t) + js, core)

    def take_d(t):
        z_wait(rel(t) + jd)
        if t == 0:
            z_copy(rel(t) + jd, zpart)
        z_copy(rel(t) + jd, core)

    def take_core(t):
        for q in range(4):
            z_wait(rel(t) + 2 * q + 1 - c)

    def scores(t, v):
        def body(h, carry):
            d0 = rel(t) + h * 4
            zb = zc[pl.ds(d0, 4), v * ROWS:(v + 1) * ROWS, :].reshape(BLK, DIM)
            n0 = pl.multiple_of(d0 * ROWS, BLK)
            acc = jnp.zeros((8, BLK), F32)
            for k0 in range(0, COLS, MB):
                cs = call[pl.ds(pl.multiple_of(j * COLS + k0, MB), MB), :]
                e = jnp.exp2(lax.dot_general(cs, zb, NT, preferred_element_type=F32) * (INV_T * LOG2E))
                e_ref[v, k0:k0 + MB, pl.ds(n0, BLK)] = e
                a_ref[v, k0:k0 + MB, pl.ds(n0, BLK)] = e * e
                acc = acc + jnp.sum(e.reshape(MB // 8, 8, BLK), axis=0)
            tot = jnp.sum(acc, axis=0, keepdims=True)
            for b in range(2):
                rbuf[0, v, j, pl.ds(d0 // 2 + b, 1), :] = tot[:, b * LANES:(b + 1) * LANES]
            return carry

        lax.fori_loop(0, 2, body, 0)

    take_f(0)
    take_s(0)
    take_z(1)
    take_z(2)
    take_d(0)
    take_z(3)
    take_f(1)
    take_s(1)
    take_core(0)
    scores(0, 0)
    take_f(2)
    take_s(2)
    take_d(1)
    scores(0, 1)
    take_f(3)
    take_s(3)
    take_core(1)
    scores(1, 0)
    take_d(2)
    scores(1, 1)
    take_d(3)
    take_core(2)
    scores(2, 0)
    scores(2, 1)
    take_core(3)
    scores(3, 0)
    scores(3, 1)

    def ar_copies(ph, v):
        buf = rbuf.at[ph, v, j]
        return [remote(buf, buf, ar_send.at[2 * ph + v, t], ar_recv.at[2 * ph + v, j], dev)
                for t, dev in enumerate(peers)]

    def ar_start(ph, v):
        for cp in ar_copies(ph, v):
            cp.start()

    def ar_wait(ph, v):
        for o in slots:
            buf = rbuf.at[ph, v, o]
            remote(buf, buf, ar_send.at[0, 0], ar_recv.at[2 * ph + v, o], me).wait_recv()
        tot = rbuf[ph, v, 0]
        for o in PEERS:
            tot = tot + rbuf[ph, v, o]
        return tot

    ar_start(0, 0)
    ar_start(0, 1)

    lane = lax.broadcasted_iota(jnp.int32, (1, LANES), 1)
    for b in range(DENSE):
        mden[pl.ds(b, 1), :] = jnp.where(lane < ROWS, mbuf[2 * b], mbuf[2 * b + 1])
    mask = mden[...]
    valid = jnp.sum(jnp.sum(mask, axis=0, keepdims=True), axis=1, keepdims=True)

    def spread(dense, slot, v):
        uden[...] = dense
        for b in range(DENSE):
            ub[slot, v, :, b * LANES:(b + 1) * LANES] = jnp.broadcast_to(uden[pl.ds(b, 1), :], (8, LANES))

    spread(mask, 0, 0)
    spread(mask, 0, 1)

    def sweep(ph, v):
        u = ub[0, v]

        def body(i, acc):
            rows = [pl.multiple_of((i * GRP + g) * 8, 8) for g in range(GRP)]
            for row in rows:
                col = jnp.sum(a_ref[v, pl.ds(row, 8), :] * u, axis=1, keepdims=True)
                vbc[v, pl.ds(row, 8), :] = jnp.broadcast_to(1.0 / (PROTOS * col), (8, LANES))
            for row in rows:
                vg = jnp.concatenate([vbc[v, pl.ds(row, 8), :]] * DENSE, axis=1)
                acc = acc + a_ref[v, pl.ds(row, 8), :] * vg
            return acc

        acc = lax.fori_loop(0, COLS // (8 * GRP), body, jnp.zeros((8, SAMPLES), F32))
        tot = jnp.sum(acc, axis=0, keepdims=True)
        for b in range(DENSE):
            rbuf[ph, v, j, pl.ds(b, 1), :] = tot[:, b * LANES:(b + 1) * LANES]

    def v_copies(v):
        buf = vall.at[v, j]
        return [remote(buf, buf, v_send.at[v, t], v_recv.at[v, j], dev) for t, dev in enumerate(peers)]

    def send_v(v):
        diag = (lax.broadcasted_iota(jnp.int32, (LANES, LANES), 0) == lax.broadcasted_iota(jnp.int32, (LANES, LANES), 1))
        for b in range(BLOCKS):
            blk = vbc[v, b * LANES:(b + 1) * LANES, :]
            vall[v, j, :, b * LANES:(b + 1) * LANES] = jnp.sum(jnp.where(diag, blk, 0.0), axis=0, keepdims=True)
        for cp in v_copies(v):
            cp.start()

    for it in range(ITERS):
        for v in range(2):
            if it > 0:
                spread(mask / (valid * ar_wait(it, v)), 0, v)
            sweep(it + 1, v)
            ar_start(it + 1, v)
            if it == ITERS - 1:
                send_v(v)
        row_scores(ROW_CUTS[it], ROW_CUTS[it + 1])
    mu = [mask / ar_wait(ITERS, v) for v in range(2)]

    gam = mask / (valid * 0.2)
    soft = [ar_wait(0, v) for v in range(2)]
    for v in range(2):
        spread(mu[v] * gam, 0, v)
        spread(gam / soft[v], 1, v)

    def unit_of(w):
        return w + par * (UNITS - 1 - 2 * w)

    def unit_ref(q, u):
        return dc_ref.at[pl.ds(pl.multiple_of(q * COLS + u * UNIT, UNIT), UNIT), :]

    def d_copy(q, u, ssem, rsem, dev):
        return remote(unit_ref(q, u), unit_ref(q, u), ssem, rsem, dev)

    def d_core(q, s, u):
        return d_copy(q, u, d_sc.at[s, u], dcore_recv.at[q // 2, u], core)

    def d_wait(q, s, u):
        d_copy(q, u, d_sf.at[0], d_recv.at[s, u], me).wait_recv()

    def own_block(k0, size):
        k0 = pl.multiple_of(k0, size)

        def body(i, acc):
            n0 = pl.multiple_of(i * BLK, BLK)
            es, vs = [], []
            for v in range(2):
                es.append(e_ref[v, pl.ds(k0, size), pl.ds(n0, BLK)].reshape(size // 8, 8, BLK))
                vs.append(jnp.concatenate([vbc[v, pl.ds(k0, size), :]] * 2, axis=1).reshape(size // 8, 8, BLK))
            for v in range(2):
                o = 1 - v
                g = (es[v] * ub[1, v, :, pl.ds(n0, BLK)][None]
                     - (es[o] * es[o] * vs[o]) * ub[0, o, :, pl.ds(n0, BLK)][None])
                zb = zc[pl.ds(i * 4, 4), v * ROWS:(v + 1) * ROWS, :].reshape(BLK, DIM)
                acc = acc + jnp.dot(g.reshape(size, BLK).astype(BF16), zb, preferred_element_type=F32)
            return acc

        acc = lax.fori_loop(0, SAMPLES // BLK, body, jnp.zeros((size, DIM), F32))
        dc_ref[pl.ds(pl.multiple_of(j * COLS + k0, size), size), :] = acc

    def send_own(w):
        u = unit_of(w)
        if w < DIRECT:
            d_copy(j, u, d_sf.at[u], d_recv.at[0, u], first).start()
        d_core(j, 0, u).start()

    def send_second(w):
        u = unit_of(w)
        d_copy(j, u, d_ss.at[u], d_recv.at[1, u], second).start()

    def take_first(w):
        u = unit_of(w)
        d_wait(jf, 0, u)
        d_copy(jf, u, d_fs.at[u], d_recv.at[2, u], second).start()
        if w < UNITS - DIRECT:
            d_copy(jf, u, d_sz.at[0, u], d_recv.at[0, u], zpart).start()
        d_core(jf, 1, u).start()

    def take_second(w):
        u = unit_of(w)
        d_wait(js, 1, u)
        if w < UNITS - DIRECT:
            d_copy(js, u, d_sz.at[1, u], d_recv.at[1, u], zpart).start()
        d_core(js, 2, u).start()

    def take_diag(w):
        u = unit_of(w)
        d_wait(jd, 2, u)
        if w < UNITS - DIRECT:
            d_copy(jd, u, d_sz.at[2, u], d_recv.at[2, u], zpart).start()
        d_core(jd, 3, u).start()

    LAG = 3

    def step(w):
        take_first(w)
        if w + LAG < DIRECT:
            send_second(w + LAG)
        take_second(w)
        if w >= LAG:
            take_diag(w - LAG)

    def own_units(b):
        own_block((b + par * (BLOCKS - 1 - 2 * b)) * LANES, LANES)
        send_own(2 * b)
        send_own(2 * b + 1)

    for w in range(2):
        own_block(unit_of(w) * UNIT, UNIT)
        send_own(w)
        send_second(w)
    own_units(1)
    send_second(2)
    early = DIRECT // 2 + 1
    for b in range(2, early):
        own_units(b)
        step(b - 2)

    sub = lax.broadcasted_iota(jnp.int32, (ROWS, LANES), 0)
    pick = lax.broadcasted_iota(jnp.int32, (ROWS, LANES), 1) == sub + ROWS * (me % 2)

    def own_rows(dense):
        uden[...] = dense
        row = jnp.broadcast_to(uden[pl.ds(me // 2, 1), :], (ROWS, LANES))
        return jnp.sum(jnp.where(pick, row, 0.0), axis=1, keepdims=True)

    gm = own_rows(gam)
    mus = [own_rows(mu[v]) for v in range(2)]
    ps = [own_rows(soft[v]) for v in range(2)]
    ips = [1.0 / p for p in ps]
    lps = [jnp.log(p) for p in ps]
    for v in range(2):
        for o in slots:
            buf = vall.at[v, o]
            remote(buf, buf, v_send.at[0, 0], v_recv.at[v, o], me).wait_recv()
    q_refs = (q1_ref, q2_ref)
    chunks = COLS // BLK

    def row_body(i, carry):
        dz, lacc = carry
        k0 = pl.multiple_of(i * BLK, BLK)
        l0 = pl.multiple_of((i % chunks) * BLK, BLK)
        ss, es, qs, gs = [], [], [], []
        for v in range(2):
            ss.append(q_refs[v][:, pl.ds(k0, BLK)] * INV_T)
            es.append(jnp.exp2(ss[v] * LOG2E))
            qs.append((es[v] * es[v]) * mus[v] * vall[v, i // chunks, :, pl.ds(l0, BLK)])
            q_refs[v][:, pl.ds(k0, BLK)] = qs[v]
        for v in range(2):
            lsum = qs[1 - v] * (ss[v] - lps[v])
            lacc = lacc + jnp.sum(lsum.reshape(ROWS // 8, 8, BLK), axis=0)
            gs.append((es[v] * ips[v] - qs[1 - v]) * gm)
        g = jnp.concatenate(gs, axis=0).astype(BF16)
        return dz + jnp.dot(g, call[pl.ds(k0, BLK), :], preferred_element_type=F32), lacc

    carry = (jnp.zeros((SLAB, DIM), F32), jnp.zeros((8, BLK), F32))
    cuts = (0, 7, 14, 20, 26, PROTOS // BLK)
    for i, (lo, hi) in enumerate(zip(cuts[:-1], cuts[1:])):
        carry = lax.fori_loop(lo, hi, row_body, carry)
        step(early - 2 + i)
    dz, lacc = carry
    dz1_ref[...] = dz[:ROWS]
    dz2_ref[...] = dz[ROWS:]
    lpart = jnp.sum(jnp.sum(lacc, axis=0, keepdims=True), axis=1, keepdims=True)
    lbuf[j] = jnp.broadcast_to(lpart, (8, LANES))
    l_copies = [remote(lbuf.at[j], lbuf.at[j], l_send.at[t], l_recv.at[j], dev) for t, dev in enumerate(peers)]
    for cp in l_copies:
        cp.start()

    for b in range(early, BLOCKS):
        own_units(b)
        step(b + len(cuts) - LAG)

    for o in slots:
        remote(lbuf.at[o], lbuf.at[o], l_send.at[0], l_recv.at[o], me).wait_recv()
    lsum = lbuf[0]
    for o in PEERS:
        lsum = lsum + lbuf[o]
    lzbuf[z] = lsum
    lz_copies = [remote(lzbuf.at[z], lzbuf.at[z], lz_send.at[t], lz_recv.at[z], dev) for t, dev in enumerate(zpeers)]
    for cp in lz_copies:
        cp.start()

    for w in range(DIRECT - LAG, DIRECT):
        take_diag(w)

    for w in reversed(range(DIRECT, UNITS)):
        u = unit_of(w)
        for s, q in ((0, jf), (1, js), (2, jd)):
            d_wait(q, s, u)
            d_core(q, s + 1, u).start()

    for o in planes[1:]:
        remote(lzbuf.at[o], lzbuf.at[o], lz_send.at[0], lz_recv.at[o], me).wait_recv()
    loss = lzbuf[0]
    for o in range(1, PLANES):
        loss = loss + lzbuf[o]
    loss_ref[...] = (-loss / (2.0 * valid))[:1, :1]

    @pl.loop(0, UNITS)
    def _(u):
        for q in range(4):
            d_copy(2 * q + 1 - c, u, d_sf.at[0], dcore_recv.at[q, u], me).wait_recv()

    for v in range(2):
        for ph in range(ITERS + 1):
            pending += ar_copies(ph, v)
        pending += v_copies(v)
    for cp in pending + l_copies + lz_copies:
        cp.wait_send()
    for w in range(UNITS):
        u = unit_of(w)
        for s in range(4):
            d_copy(j, u, d_sc.at[s, u], dcore_recv.at[0, u], core).wait_send()
        if w < DIRECT:
            d_copy(j, u, d_sf.at[u], d_recv.at[0, u], first).wait_send()
            d_copy(j, u, d_ss.at[u], d_recv.at[1, u], second).wait_send()
            d_copy(jf, u, d_fs.at[u], d_recv.at[2, u], second).wait_send()
        if w < UNITS - DIRECT:
            for s in range(3):
                d_copy(j, u, d_sz.at[s, u], d_recv.at[s, u], zpart).wait_send()


STORE = (4, 4, 1, 1, 1, 8)


def store_kernel(*refs):
    results = len(STORE)
    sem = refs[2 * results]
    copies = []
    for i, pieces in enumerate(STORE):
        src, dst = refs[i], refs[results + i]
        rows = src.shape[0] // pieces
        for p in range(pieces):
            part = pl.ds(p * rows, rows)
            copies.append(pltpu.make_async_copy(src.at[part, :], dst.at[part, :], sem.at[len(copies)]))
            copies[-1].start()
    for cp in copies:
        cp.wait()


def solution(mesh):
    def local_step(view_one, view_two, protos, valid_mask):
        dma = pltpu.SemaphoreType.DMA
        outs = pl.pallas_call(
            kernel,
            out_shape=[
                pltpu.VMEM((ROWS, PROTOS), F32),
                pltpu.VMEM((ROWS, PROTOS), F32),
                pltpu.VMEM((1, 1), F32),
                pltpu.VMEM((ROWS, DIM), F32),
                pltpu.VMEM((ROWS, DIM), F32),
                pltpu.VMEM((PROTOS, DIM), F32),
            ],
            in_specs=[pl.BlockSpec(memory_space=pl.ANY)] * 4,
            out_specs=[pl.BlockSpec(memory_space=pltpu.VMEM)] * 6,
            scratch_shapes=[
                pltpu.VMEM((DEVS, SLAB, DIM), BF16),
                pltpu.VMEM((1, ROWS), jnp.int32),
                pltpu.VMEM((DEVS, 1, LANES), F32),
                pltpu.VMEM((PROTOS, DIM), BF16),
                pltpu.VMEM((2, COLS, SAMPLES), F32),
                pltpu.VMEM((2, COLS, SAMPLES), F32),
                pltpu.VMEM((2, COLS, LANES), F32),
                pltpu.VMEM((DENSE, LANES), F32),
                pltpu.VMEM((DENSE, LANES), F32),
                pltpu.VMEM((2, 2, 8, SAMPLES), F32),
                pltpu.VMEM((ITERS + 1, 2, PLANE, DENSE, LANES), F32),
                pltpu.VMEM((2, PLANE, 1, COLS), F32),
                pltpu.VMEM((PLANE, 8, LANES), F32),
                pltpu.VMEM((PLANES, 8, LANES), F32),
                dma((4,)), dma((DEVS - 1,)), dma((DEVS,)), dma((DEVS - 1,)), dma((DEVS,)),
                dma((2 * ITERS + 2, PLANE - 1)), dma((2 * ITERS + 2, PLANE)),
                dma((2, PLANE - 1)), dma((2, PLANE)),
                dma((PLANE - 1,)), dma((PLANE,)), dma((PLANES - 1,)), dma((PLANES,)),
                dma((3, UNITS)), dma((4, UNITS)), dma((UNITS,)), dma((UNITS,)), dma((4, UNITS)),
                dma((UNITS,)), dma((3, UNITS)),
            ],
            compiler_params=pltpu.CompilerParams(
                collective_id=0, has_side_effects=True, vmem_limit_bytes=48 << 20),
        )(view_one, view_two, valid_mask.reshape(1, ROWS), protos)
        outs = pl.pallas_call(
            store_kernel,
            out_shape=[jax.ShapeDtypeStruct(o.shape, o.dtype) for o in outs],
            in_specs=[pl.BlockSpec(memory_space=pltpu.VMEM)] * len(STORE),
            out_specs=[pl.BlockSpec(memory_space=pl.ANY)] * len(STORE),
            scratch_shapes=[dma((sum(STORE),))],
            compiler_params=pltpu.CompilerParams(vmem_limit_bytes=4 << 20),
        )(*[pltpu.with_memory_space_constraint(o, pltpu.VMEM) for o in outs])
        q1, q2, loss, dz1, dz2, dc = outs
        return q1, q2, loss.reshape(()), dz1, dz2, dc

    return jax.shard_map(
        local_step,
        mesh=mesh,
        in_specs=(P("data", None), P("data", None), P(None, None), P("data")),
        out_specs=(P("data", None), P("data", None), P(), P("data", None), P("data", None), P(None, None)),
        check_vma=False,
    )
```

time: 104 us -> 81.8 us (0.79)
  Pallas kernels: 103 us -> 81 us
    pallas_call x1, Pallas kernels: 97.7 us -> 75.6 us  [local_step(): pl.pallas_call(kernel, out_shape=[pltpu.VMEM((ROWS, PROTOS), F32), pltpu....]
where the time goes in v3:
time: 81.8 us; the launch traced here: 81.7 us
  Pallas kernels  81 us (99%)
    pallas_call x1, Pallas kernels, local_step(): pl.pallas_call(kernel, out_shape=[pltpu.VMEM((ROWS, PROTOS), F32), pltpu....  75.6 us
    pallas_call x1, Pallas kernels, local_step(): pl.pallas_call(store_kernel, out_shape=[jax.ShapeDtypeStruct(o.shape, o.d...  5.4 us

profile of v3, /device:TPU:0, one launch (start us, length us, event | category | flops | bytes accessed | tf_op | source)
XLA Modules:
  0.0 81.7 jit_solution(8520754402076437849)
XLA Ops:
  0.6 75.6 %shard_map.91 = (f32[64,8192]{1,0:T(8,128)S(1)}, f32[64,8192]{1,0:T(8,128)S(1)}, f32[1,1]{1,0:T(1,128)}, f32[64,256]{1,0:T(8,128)S(1)}, f32[64,256]{1,0:T(8,128)S(1)}, /*index=5*/f32[8192,256]{1,0:T(8,128)S(1)}) custom-call(bf16[64,256]{1,0:T(8,128)(2,1)} %v1_hbm.1, bf16[64,256]{1,0:T(8,128)(2,1)} %v2_hbm.1, s32[1,64]{1,0:T(1,128)} %bitcast.2, ...), custom_call_target="tpu_custom_call" | custom-call | tf_op jit(solution)/shard_map/pallas_call | solution.py:499
  76.3 5.4 %shard_map.92 = (f32[64,8192]{1,0:T(8,128)}, f32[64,8192]{1,0:T(8,128)}, f32[1,1]{1,0:T(1,128)}, f32[64,256]{1,0:T(8,128)}, f32[64,256]{1,0:T(8,128)}, /*index=5*/f32[8192,256]{1,0:T(8,128)}) custom-call(f32[64,8192]{1,0:T(8,128)S(1)} %get-tuple-element.18.refs_0_, f32[64,8192]{1,0:T(8,128)S(1)} %get-tuple-element.19.refs_1_, ...), custom_call_target="tpu_custom_call" | custom-call | tf_op jit(solution)/shard_map/pallas_call | solution.py:536

commit v4 on v3

--- a/solution.py
+++ b/solution.py
@@ -21,6 +21,7 @@
 ITERS = 3
 LANES = 128
 PLANES = DEVS // PLANE
+CHIPS = PLANE // 2
 PEERS = range(1, PLANE)
 BLK = 2 * LANES
 DENSE = SAMPLES // LANES
@@ -29,15 +30,19 @@
 UNITS = COLS // UNIT
 BLOCKS = COLS // LANES
 DIRECT = 11
+KDEPTH = 1024
+RCOLS = 1024
+LAG = 3
+QCOLS = 512
 GRP = 32
 LOG2E = 1.4426950408889634
-ROW_CUTS = (5, 11, 17, 32)
+ROW_CUTS = (1, 3, 5, 7, 8)
 NT = (((1,), (1,)), ((), ()))
 
 
 def kernel(v1_hbm, v2_hbm, mk_hbm, c_hbm,
            q1_ref, q2_ref, loss_ref, dz1_ref, dz2_ref, dc_ref,
-           zc, mi, mbuf, call, e_ref, a_ref, vbc, mden, uden, ub, rbuf, vall, lbuf, lzbuf,
+           zc, mi, mbuf, call, a_ref, vbc, mden, uden, ub, rbuf, vall, lbuf, lzbuf,
            lsem, z_send, z_recv, m_send, m_recv, ar_send, ar_recv, v_send, v_recv,
            l_send, l_recv, lz_send, lz_recv,
            d_recv, dcore_recv, d_sf, d_ss, d_sc, d_fs, d_sz):
@@ -53,6 +58,7 @@
     jf = jx + c * (jy - jx)
     js = jy + c * (jx - jy)
     core = me + 1 - 2 * c
+    own_slot = z * PLANE + c * CHIPS + j // 2
     first = z * PLANE + jf
     second = z * PLANE + js
     par = z % 2
@@ -67,8 +73,8 @@
         pl.semaphore_signal(barrier, inc=1, device_id=(dev,), device_id_type=MESH)
 
     own = [
-        pltpu.make_async_copy(v1_hbm, zc.at[me, pl.ds(0, ROWS), :], lsem.at[0]),
-        pltpu.make_async_copy(v2_hbm, zc.at[me, pl.ds(ROWS, ROWS), :], lsem.at[1]),
+        pltpu.make_async_copy(v1_hbm, zc.at[own_slot, pl.ds(0, ROWS), :], lsem.at[0]),
+        pltpu.make_async_copy(v2_hbm, zc.at[own_slot, pl.ds(ROWS, ROWS), :], lsem.at[1]),
         pltpu.make_async_copy(mk_hbm, mi, lsem.at[2]),
     ]
     for cp in own:
@@ -78,7 +84,7 @@
     for cp in own:
         cp.wait()
     mrow = mi[...].astype(F32)
-    mbuf[me] = jnp.concatenate([mrow, mrow], axis=1)
+    mbuf[own_slot] = jnp.concatenate([mrow, mrow], axis=1)
     pl.semaphore_wait(barrier, len(peers + zpeers))
 
     def remote(src, dst, ssem, rsem, dev):
@@ -98,102 +104,93 @@
         remote(zc.at[i], zc.at[i], z_send.at[0], z_recv.at[i], me).wait_recv()
         remote(mbuf.at[i], mbuf.at[i], m_send.at[0], m_recv.at[i], me).wait_recv()
 
-    def rel(t):
-        return planes[t] * PLANE
-
     def row_scores(lo, hi):
         def body(i, carry):
-            k0 = pl.multiple_of(i * BLK, BLK)
-            rs = lax.dot_general(zc[me], call[pl.ds(k0, BLK), :], NT, preferred_element_type=F32)
-            q1_ref[:, pl.ds(k0, BLK)] = rs[:ROWS]
-            q2_ref[:, pl.ds(k0, BLK)] = rs[ROWS:]
+            k0 = pl.multiple_of(i * RCOLS, RCOLS)
+            rs = lax.dot_general(zc[own_slot], call[pl.ds(k0, RCOLS), :], NT, preferred_element_type=F32)
+            q1_ref[:, pl.ds(k0, RCOLS)] = rs[:ROWS]
+            q2_ref[:, pl.ds(k0, RCOLS)] = rs[ROWS:]
             return carry
 
         lax.fori_loop(lo, hi, body, 0)
 
-    z_copy(me, first)
-    z_copy(me, second)
+    z_copy(own_slot, first)
+    z_copy(own_slot, second)
     for dev in zpeers:
-        z_copy(me, dev)
-    z_copy(me, core)
+        z_copy(own_slot, dev)
+    z_copy(own_slot, core)
     c_copy.wait()
     row_scores(0, ROW_CUTS[0])
 
+    def take(t, k, *devs):
+        i = planes[t] * PLANE + c * CHIPS + k // 2
+        z_wait(i)
+        for dev in devs + (core,):
+            z_copy(i, dev)
+
     def take_z(t):
-        z_wait(rel(t) + j)
-        z_copy(rel(t) + j, first)
-        if t != 1:
-            z_copy(rel(t) + j, second)
-        z_copy(rel(t) + j, core)
+        take(t, j, *((first,) if t == 1 else (first, second)))
 
     def take_f(t):
-        z_wait(rel(t) + jf)
-        if t != 1:
-            z_copy(rel(t) + jf, second)
-        z_copy(rel(t) + jf, core)
+        take(t, jf, *(() if t == 1 else (second,)))
 
     def take_s(t):
-        z_wait(rel(t) + js)
-        if t == 0:
-            z_copy(rel(t) + js, zpart)
-        z_copy(rel(t) + js, core)
+        take(t, js, *((zpart,) if t == 0 else ()))
 
     def take_d(t):
-        z_wait(rel(t) + jd)
-        if t == 0:
-            z_copy(rel(t) + jd, zpart)
-        z_copy(rel(t) + jd, core)
+        take(t, jd, *((zpart,) if t == 0 else ()))
 
     def take_core(t):
-        for q in range(4):
-            z_wait(rel(t) + 2 * q + 1 - c)
-
-    def scores(t, v):
-        def body(h, carry):
-            d0 = rel(t) + h * 4
-            zb = zc[pl.ds(d0, 4), v * ROWS:(v + 1) * ROWS, :].reshape(BLK, DIM)
-            n0 = pl.multiple_of(d0 * ROWS, BLK)
+        for q in range(CHIPS):
+            z_wait(planes[t] * PLANE + (1 - c) * CHIPS + q)
+
+    def scores(t, k):
+        d0 = planes[t] * PLANE + k * CHIPS
+        n0 = pl.multiple_of(d0 * ROWS, BLK)
+
+        for v in range(2):
+            zb = zc[pl.ds(d0, CHIPS), v * ROWS:(v + 1) * ROWS, :].reshape(BLK, DIM)
             acc = jnp.zeros((8, BLK), F32)
             for k0 in range(0, COLS, MB):
                 cs = call[pl.ds(pl.multiple_of(j * COLS + k0, MB), MB), :]
                 e = jnp.exp2(lax.dot_general(cs, zb, NT, preferred_element_type=F32) * (INV_T * LOG2E))
-                e_ref[v, k0:k0 + MB, pl.ds(n0, BLK)] = e
                 a_ref[v, k0:k0 + MB, pl.ds(n0, BLK)] = e * e
                 acc = acc + jnp.sum(e.reshape(MB // 8, 8, BLK), axis=0)
             tot = jnp.sum(acc, axis=0, keepdims=True)
             for b in range(2):
                 rbuf[0, v, j, pl.ds(d0 // 2 + b, 1), :] = tot[:, b * LANES:(b + 1) * LANES]
-            return carry
-
-        lax.fori_loop(0, 2, body, 0)
+
+    def own_scores(t):
+        scores(t, c)
+
+    def other_scores(t):
+        take_core(t)
+        scores(t, 1 - c)
 
     take_f(0)
     take_s(0)
     take_z(1)
+    row_scores(ROW_CUTS[0], ROW_CUTS[1])
     take_z(2)
     take_d(0)
     take_z(3)
     take_f(1)
     take_s(1)
-    take_core(0)
-    scores(0, 0)
+    own_scores(0)
     take_f(2)
     take_s(2)
     take_d(1)
-    scores(0, 1)
+    own_scores(1)
+    other_scores(0)
     take_f(3)
     take_s(3)
-    take_core(1)
-    scores(1, 0)
     take_d(2)
-    scores(1, 1)
+    own_scores(2)
+    other_scores(1)
     take_d(3)
-    take_core(2)
-    scores(2, 0)
-    scores(2, 1)
-    take_core(3)
-    scores(3, 0)
-    scores(3, 1)
+    own_scores(3)
+    other_scores(2)
+    other_scores(3)
 
     def ar_copies(ph, v):
         buf = rbuf.at[ph, v, j]
@@ -268,13 +265,11 @@
             ar_start(it + 1, v)
             if it == ITERS - 1:
                 send_v(v)
-        row_scores(ROW_CUTS[it], ROW_CUTS[it + 1])
-    mu = [mask / ar_wait(ITERS, v) for v in range(2)]
+        row_scores(ROW_CUTS[it + 1], ROW_CUTS[it + 2])
 
     gam = mask / (valid * 0.2)
     soft = [ar_wait(0, v) for v in range(2)]
     for v in range(2):
-        spread(mu[v] * gam, 0, v)
         spread(gam / soft[v], 1, v)
 
     def unit_of(w):
@@ -292,25 +287,29 @@
     def d_wait(q, s, u):
         d_copy(q, u, d_sf.at[0], d_recv.at[s, u], me).wait_recv()
 
-    def own_block(k0, size):
+    def grad_part(k0, size, v, acc):
         k0 = pl.multiple_of(k0, size)
+        o = 1 - v
+
+        wide = KDEPTH // BLK
+        devs = KDEPTH // ROWS
 
         def body(i, acc):
-            n0 = pl.multiple_of(i * BLK, BLK)
-            es, vs = [], []
-            for v in range(2):
-                es.append(e_ref[v, pl.ds(k0, size), pl.ds(n0, BLK)].reshape(size // 8, 8, BLK))
-                vs.append(jnp.concatenate([vbc[v, pl.ds(k0, size), :]] * 2, axis=1).reshape(size // 8, 8, BLK))
-            for v in range(2):
-                o = 1 - v
-                g = (es[v] * ub[1, v, :, pl.ds(n0, BLK)][None]
-                     - (es[o] * es[o] * vs[o]) * ub[0, o, :, pl.ds(n0, BLK)][None])
-                zb = zc[pl.ds(i * 4, 4), v * ROWS:(v + 1) * ROWS, :].reshape(BLK, DIM)
-                acc = acc + jnp.dot(g.reshape(size, BLK).astype(BF16), zb, preferred_element_type=F32)
-            return acc
-
-        acc = lax.fori_loop(0, SAMPLES // BLK, body, jnp.zeros((size, DIM), F32))
-        dc_ref[pl.ds(pl.multiple_of(j * COLS + k0, size), size), :] = acc
+            n0 = pl.multiple_of(i * KDEPTH, KDEPTH)
+            a = a_ref[v, pl.ds(k0, size), pl.ds(n0, KDEPTH)].reshape(size // 8, 8, KDEPTH)
+            ao = a_ref[o, pl.ds(k0, size), pl.ds(n0, KDEPTH)].reshape(size // 8, 8, KDEPTH)
+            vo = jnp.concatenate([vbc[o, pl.ds(k0, size), :]] * (2 * wide), axis=1).reshape(size // 8, 8, KDEPTH)
+            g = (a * lax.rsqrt(a)) * ub[1, v, :, pl.ds(n0, KDEPTH)][None] - (ao * vo) * ub[0, o, :, pl.ds(n0, KDEPTH)][None]
+            zb = zc[pl.ds(i * devs, devs), v * ROWS:(v + 1) * ROWS, :].reshape(KDEPTH, DIM)
+            return acc + jnp.dot(g.reshape(size, KDEPTH).astype(BF16), zb, preferred_element_type=F32)
+
+        return lax.fori_loop(0, SAMPLES // KDEPTH, body, acc)
+
+    def grad_first(k0, size):
+        return grad_part(k0, size, 1, jnp.zeros((size, DIM), F32))
+
+    def grad_rest(k0, size, acc):
+        dc_ref[pl.ds(pl.multiple_of(j * COLS + k0, size), size), :] = grad_part(k0, size, 0, acc)
 
     def send_own(w):
         u = unit_of(w)
@@ -329,6 +328,8 @@
         if w < UNITS - DIRECT:
             d_copy(jf, u, d_sz.at[0, u], d_recv.at[0, u], zpart).start()
         d_core(jf, 1, u).start()
+        if w + LAG < DIRECT:
+            send_second(w + LAG)
 
     def take_second(w):
         u = unit_of(w)
@@ -344,38 +345,31 @@
             d_copy(jd, u, d_sz.at[2, u], d_recv.at[2, u], zpart).start()
         d_core(jd, 3, u).start()
 
-    LAG = 3
-
-    def step(w):
-        take_first(w)
-        if w + LAG < DIRECT:
-            send_second(w + LAG)
-        take_second(w)
-        if w >= LAG:
-            take_diag(w - LAG)
-
     def own_units(b):
-        own_block((b + par * (BLOCKS - 1 - 2 * b)) * LANES, LANES)
+        k0 = (b + par * (BLOCKS - 1 - 2 * b)) * LANES
+        grad_rest(k0, LANES, grad_first(k0, LANES))
         send_own(2 * b)
         send_own(2 * b + 1)
 
+    mu = [mask / ar_wait(ITERS, 0)]
+    spread(mu[0] * gam, 0, 0)
+    parts = [grad_first(unit_of(w) * UNIT, UNIT) for w in range(2)]
+    mu.append(mask / ar_wait(ITERS, 1))
+    spread(mu[1] * gam, 0, 1)
     for w in range(2):
-        own_block(unit_of(w) * UNIT, UNIT)
+        grad_rest(unit_of(w) * UNIT, UNIT, parts[w])
         send_own(w)
         send_second(w)
     own_units(1)
     send_second(2)
-    early = DIRECT // 2 + 1
-    for b in range(2, early):
-        own_units(b)
-        step(b - 2)
+    own_units(2)
 
     sub = lax.broadcasted_iota(jnp.int32, (ROWS, LANES), 0)
-    pick = lax.broadcasted_iota(jnp.int32, (ROWS, LANES), 1) == sub + ROWS * (me % 2)
+    pick = lax.broadcasted_iota(jnp.int32, (ROWS, LANES), 1) == sub + ROWS * (own_slot % 2)
 
     def own_rows(dense):
         uden[...] = dense
-        row = jnp.broadcast_to(uden[pl.ds(me // 2, 1), :], (ROWS, LANES))
+        row = jnp.broadcast_to(uden[pl.ds(own_slot // 2, 1), :], (ROWS, LANES))
         return jnp.sum(jnp.where(pick, row, 0.0), axis=1, keepdims=True)
 
     gm = own_rows(gam)
@@ -388,31 +382,47 @@
             buf = vall.at[v, o]
             remote(buf, buf, v_send.at[0, 0], v_recv.at[v, o], me).wait_recv()
     q_refs = (q1_ref, q2_ref)
-    chunks = COLS // BLK
+    chunks = COLS // QCOLS
 
     def row_body(i, carry):
         dz, lacc = carry
-        k0 = pl.multiple_of(i * BLK, BLK)
-        l0 = pl.multiple_of((i % chunks) * BLK, BLK)
+        k0 = pl.multiple_of(i * QCOLS, QCOLS)
+        l0 = pl.multiple_of((i % chunks) * QCOLS, QCOLS)
         ss, es, qs, gs = [], [], [], []
         for v in range(2):
-            ss.append(q_refs[v][:, pl.ds(k0, BLK)] * INV_T)
+            ss.append(q_refs[v][:, pl.ds(k0, QCOLS)] * INV_T)
             es.append(jnp.exp2(ss[v] * LOG2E))
-            qs.append((es[v] * es[v]) * mus[v] * vall[v, i // chunks, :, pl.ds(l0, BLK)])
-            q_refs[v][:, pl.ds(k0, BLK)] = qs[v]
+            qs.append((es[v] * es[v]) * mus[v] * vall[v, i // chunks, :, pl.ds(l0, QCOLS)])
+            q_refs[v][:, pl.ds(k0, QCOLS)] = qs[v]
         for v in range(2):
             lsum = qs[1 - v] * (ss[v] - lps[v])
-            lacc = lacc + jnp.sum(lsum.reshape(ROWS // 8, 8, BLK), axis=0)
+            lacc = lacc + jnp.sum(lsum.reshape(ROWS // 8, 8, QCOLS), axis=0)
             gs.append((es[v] * ips[v] - qs[1 - v]) * gm)
         g = jnp.concatenate(gs, axis=0).astype(BF16)
-        return dz + jnp.dot(g, call[pl.ds(k0, BLK), :], preferred_element_type=F32), lacc
-
-    carry = (jnp.zeros((SLAB, DIM), F32), jnp.zeros((8, BLK), F32))
-    cuts = (0, 7, 14, 20, 26, PROTOS // BLK)
-    for i, (lo, hi) in enumerate(zip(cuts[:-1], cuts[1:])):
-        carry = lax.fori_loop(lo, hi, row_body, carry)
-        step(early - 2 + i)
-    dz, lacc = carry
+        return dz + jnp.dot(g, call[pl.ds(k0, QCOLS), :], preferred_element_type=F32), lacc
+
+    carry = (jnp.zeros((SLAB, DIM), F32), jnp.zeros((8, QCOLS), F32))
+    cuts = (0, 4, 7, 10, 13, PROTOS // QCOLS)
+
+    def row_part(i, carry):
+        return lax.fori_loop(cuts[i], cuts[i + 1], row_body, carry)
+
+    carry = row_part(0, carry)
+    take_first(0)
+    take_second(0)
+    carry = row_part(1, carry)
+    take_first(1)
+    take_second(1)
+    own_units(3)
+    take_first(2)
+    take_second(2)
+    carry = row_part(2, carry)
+    take_first(3)
+    take_diag(0)
+    carry = row_part(3, carry)
+    take_first(4)
+    take_second(3)
+    dz, lacc = row_part(4, carry)
     dz1_ref[...] = dz[:ROWS]
     dz2_ref[...] = dz[ROWS:]
     lpart = jnp.sum(jnp.sum(lacc, axis=0, keepdims=True), axis=1, keepdims=True)
@@ -420,10 +430,22 @@
     l_copies = [remote(lbuf.at[j], lbuf.at[j], l_send.at[t], l_recv.at[j], dev) for t, dev in enumerate(peers)]
     for cp in l_copies:
         cp.start()
-
-    for b in range(early, BLOCKS):
-        own_units(b)
-        step(b + len(cuts) - LAG)
+    own_units(4)
+    take_first(5)
+    take_diag(1)
+    take_first(6)
+    take_second(4)
+    own_units(5)
+    take_first(7)
+    take_diag(2)
+    take_first(8)
+    take_second(5)
+    own_units(6)
+    take_first(9)
+    take_diag(3)
+    take_first(10)
+    take_second(6)
+    take_diag(4)
 
     for o in slots:
         remote(lbuf.at[o], lbuf.at[o], l_send.at[0], l_recv.at[o], me).wait_recv()
@@ -435,8 +457,12 @@
     for cp in lz_copies:
         cp.start()
 
-    for w in range(DIRECT - LAG, DIRECT):
-        take_diag(w)
+    own_units(7)
+    for w in range(7, DIRECT):
+        take_second(w)
+        take_diag(w - 2)
+    take_diag(DIRECT - 2)
+    take_diag(DIRECT - 1)
 
     for w in reversed(range(DIRECT, UNITS)):
         u = unit_of(w)
@@ -513,7 +539,6 @@
                 pltpu.VMEM((1, ROWS), jnp.int32),
                 pltpu.VMEM((DEVS, 1, LANES), F32),
                 pltpu.VMEM((PROTOS, DIM), BF16),
-                pltpu.VMEM((2, COLS, SAMPLES), F32),
                 pltpu.VMEM((2, COLS, SAMPLES), F32),
                 pltpu.VMEM((2, COLS, LANES), F32),
                 pltpu.VMEM((DENSE, LANES), F32),

time: 81.8 us -> 77.7 us (0.950)
  Pallas kernels: 81 us -> 76.9 us
    pallas_call x1, Pallas kernels: 75.6 us -> 71.5 us  [local_step(): pl.pallas_call(kernel, out_shape=[pltpu.VMEM((ROWS, PROTOS), F32), pltpu....]
where the time goes in v4:
time: 77.7 us; the launch traced here: 77.6 us
  Pallas kernels  76.9 us (99%)
    pallas_call x1, Pallas kernels, local_step(): pl.pallas_call(kernel, out_shape=[pltpu.VMEM((ROWS, PROTOS), F32), pltpu....  71.5 us
    pallas_call x1, Pallas kernels, local_step(): pl.pallas_call(store_kernel, out_shape=[jax.ShapeDtypeStruct(o.shape, o.d...  5.4 us

profile of v4, /device:TPU:0, one launch (start us, length us, event | category | flops | bytes accessed | tf_op | source)
XLA Modules:
  0.0 77.6 jit_solution(3445535422420261989)
XLA Ops:
  0.6 71.5 %shard_map.91 = (f32[64,8192]{1,0:T(8,128)S(1)}, f32[64,8192]{1,0:T(8,128)S(1)}, f32[1,1]{1,0:T(1,128)}, f32[64,256]{1,0:T(8,128)S(1)}, f32[64,256]{1,0:T(8,128)S(1)}, /*index=5*/f32[8192,256]{1,0:T(8,128)S(1)}) custom-call(bf16[64,256]{1,0:T(8,128)(2,1)} %v1_hbm.1, bf16[64,256]{1,0:T(8,128)(2,1)} %v2_hbm.1, s32[1,64]{1,0:T(1,128)} %bitcast.2, ...), custom_call_target="tpu_custom_call" | custom-call | tf_op jit(solution)/shard_map/pallas_call | solution.py:525
  72.2 5.4 %shard_map.92 = (f32[64,8192]{1,0:T(8,128)}, f32[64,8192]{1,0:T(8,128)}, f32[1,1]{1,0:T(1,128)}, f32[64,256]{1,0:T(8,128)}, f32[64,256]{1,0:T(8,128)}, /*index=5*/f32[8192,256]{1,0:T(8,128)}) custom-call(f32[64,8192]{1,0:T(8,128)S(1)} %get-tuple-element.18.refs_0_, f32[64,8192]{1,0:T(8,128)S(1)} %get-tuple-element.19.refs_1_, ...), custom_call_target="tpu_custom_call" | custom-call | tf_op jit(solution)/shard_map/pallas_call | solution.py:561

commit v5 on v4

--- a/solution.py
+++ b/solution.py
@@ -29,7 +29,10 @@
 UNIT = 64
 UNITS = COLS // UNIT
 BLOCKS = COLS // LANES
-DIRECT = 11
+FIRST = 12
+SECOND = 11
+DIAG = 4
+LOCAL = COLS - 2 * DIAG * UNIT
 KDEPTH = 1024
 RCOLS = 1024
 LAG = 3
@@ -37,15 +40,14 @@
 GRP = 32
 LOG2E = 1.4426950408889634
 ROW_CUTS = (1, 3, 5, 7, 8)
+DIAG_CUTS = (0, 4, 5, 8)
 NT = (((1,), (1,)), ((), ()))
 
 
 def kernel(v1_hbm, v2_hbm, mk_hbm, c_hbm,
            q1_ref, q2_ref, loss_ref, dz1_ref, dz2_ref, dc_ref,
-           zc, mi, mbuf, call, a_ref, vbc, mden, uden, ub, rbuf, vall, lbuf, lzbuf,
-           lsem, z_send, z_recv, m_send, m_recv, ar_send, ar_recv, v_send, v_recv,
-           l_send, l_recv, lz_send, lz_recv,
-           d_recv, dcore_recv, d_sf, d_ss, d_sc, d_fs, d_sz):
+           zc, mi, mbuf, call, a_ref, ad_ref, vbc, vd, mden, uden, ub, rbuf, vall, lbuf, lzbuf,
+           lsem, z_send, z_recv, zcore_recv, m_recv, mcore_recv, ar_send, ar_recv, v_recv, l_recv, d_recv, d_send):
     me = lax.axis_index("data")
     z = me // PLANE
     j = me % PLANE
@@ -65,7 +67,6 @@
     planes = (z, z + 1 - 2 * par, z + 2 - PLANES * (z // 2), PLANES - 1 - z)
     zpart = planes[1] * PLANE + j
     peers = [z * PLANE + (j + t) % PLANE for t in PEERS]
-    slots = [(j + t) % PLANE for t in PEERS]
     zpeers = [p * PLANE + j for p in planes[1:]]
 
     barrier = pltpu.get_barrier_semaphore()
@@ -91,18 +92,23 @@
         return pltpu.make_async_remote_copy(src_ref=src, dst_ref=dst, send_sem=ssem, recv_sem=rsem,
                                             device_id=(dev,), device_id_type=MESH)
 
-    pending = []
+    def wait_in(buf, rsem):
+        remote(buf, buf, lsem.at[0], rsem, me).wait_recv()
+
+    def wait_out(buf, ssem):
+        remote(buf, buf, ssem, lsem.at[0], me).wait_send()
 
     def z_copy(i, dev):
-        k = len(pending) // 2
-        for cp in (remote(zc.at[i], zc.at[i], z_send.at[k], z_recv.at[i], dev),
-                   remote(mbuf.at[i], mbuf.at[i], m_send.at[k], m_recv.at[i], dev)):
-            pending.append(cp)
-            cp.start()
+        remote(zc.at[i], zc.at[i], z_send.at[0], z_recv.at[i], dev).start()
+        remote(mbuf.at[i], mbuf.at[i], z_send.at[1], m_recv.at[i], dev).start()
+
+    def z_core(i, p):
+        remote(zc.at[i], zc.at[i], z_send.at[0], zcore_recv.at[p], core).start()
+        remote(mbuf.at[i], mbuf.at[i], z_send.at[1], mcore_recv.at[p], core).start()
 
     def z_wait(i):
-        remote(zc.at[i], zc.at[i], z_send.at[0], z_recv.at[i], me).wait_recv()
-        remote(mbuf.at[i], mbuf.at[i], m_send.at[0], m_recv.at[i], me).wait_recv()
+        wait_in(zc.at[i], z_recv.at[i])
+        wait_in(mbuf.at[i], m_recv.at[i])
 
     def row_scores(lo, hi):
         def body(i, carry):
@@ -118,15 +124,16 @@
     z_copy(own_slot, second)
     for dev in zpeers:
         z_copy(own_slot, dev)
-    z_copy(own_slot, core)
+    z_core(own_slot, z)
     c_copy.wait()
     row_scores(0, ROW_CUTS[0])
 
     def take(t, k, *devs):
         i = planes[t] * PLANE + c * CHIPS + k // 2
         z_wait(i)
-        for dev in devs + (core,):
+        for dev in devs:
             z_copy(i, dev)
+        z_core(i, planes[t])
 
     def take_z(t):
         take(t, j, *((first,) if t == 1 else (first, second)))
@@ -141,8 +148,9 @@
         take(t, jd, *((zpart,) if t == 0 else ()))
 
     def take_core(t):
-        for q in range(CHIPS):
-            z_wait(planes[t] * PLANE + (1 - c) * CHIPS + q)
+        part = pl.ds(planes[t] * PLANE + (1 - c) * CHIPS, CHIPS)
+        wait_in(zc.at[part], zcore_recv.at[planes[t]])
+        wait_in(mbuf.at[part], mcore_recv.at[planes[t]])
 
     def scores(t, k):
         d0 = planes[t] * PLANE + k * CHIPS
@@ -192,19 +200,17 @@
     other_scores(2)
     other_scores(3)
 
-    def ar_copies(ph, v):
-        buf = rbuf.at[ph, v, j]
-        return [remote(buf, buf, ar_send.at[2 * ph + v, t], ar_recv.at[2 * ph + v, j], dev)
-                for t, dev in enumerate(peers)]
+    def to_plane(buf, ssem, rsem):
+        for dev in peers:
+            remote(buf, buf, ssem, rsem, dev).start()
+
+    others = pl.ds(0, PLANE - 1)
 
     def ar_start(ph, v):
-        for cp in ar_copies(ph, v):
-            cp.start()
+        to_plane(rbuf.at[ph, v, j], ar_send.at[0], ar_recv.at[2 * ph + v])
 
     def ar_wait(ph, v):
-        for o in slots:
-            buf = rbuf.at[ph, v, o]
-            remote(buf, buf, ar_send.at[0, 0], ar_recv.at[2 * ph + v, o], me).wait_recv()
+        wait_in(rbuf.at[ph, v, others], ar_recv.at[2 * ph + v])
         tot = rbuf[ph, v, 0]
         for o in PEERS:
             tot = tot + rbuf[ph, v, o]
@@ -245,17 +251,25 @@
         for b in range(DENSE):
             rbuf[ph, v, j, pl.ds(b, 1), :] = tot[:, b * LANES:(b + 1) * LANES]
 
-    def v_copies(v):
-        buf = vall.at[v, j]
-        return [remote(buf, buf, v_send.at[v, t], v_recv.at[v, j], dev) for t, dev in enumerate(peers)]
-
     def send_v(v):
         diag = (lax.broadcasted_iota(jnp.int32, (LANES, LANES), 0) == lax.broadcasted_iota(jnp.int32, (LANES, LANES), 1))
         for b in range(BLOCKS):
             blk = vbc[v, b * LANES:(b + 1) * LANES, :]
             vall[v, j, :, b * LANES:(b + 1) * LANES] = jnp.sum(jnp.where(diag, blk, 0.0), axis=0, keepdims=True)
-        for cp in v_copies(v):
-            cp.start()
+        to_plane(vall.at[v, j], ar_send.at[1], v_recv.at[v])
+
+    def diag_scores(lo, hi):
+        def body(i, carry):
+            n0 = pl.multiple_of(i * BLK, BLK)
+            for v in range(2):
+                zb = zc[pl.ds(i * CHIPS, CHIPS), v * ROWS:(v + 1) * ROWS, :].reshape(BLK, DIM)
+                for k0 in range(0, LOCAL, MB):
+                    cs = call[pl.ds(pl.multiple_of(jd * COLS + DIAG * UNIT + k0, MB), MB), :]
+                    e = jnp.exp2(lax.dot_general(cs, zb, NT, preferred_element_type=F32) * (INV_T * LOG2E))
+                    ad_ref[v, k0:k0 + MB, pl.ds(n0, BLK)] = e * e
+            return carry
+
+        lax.fori_loop(lo, hi, body, 0)
 
     for it in range(ITERS):
         for v in range(2):
@@ -266,6 +280,7 @@
             if it == ITERS - 1:
                 send_v(v)
         row_scores(ROW_CUTS[it + 1], ROW_CUTS[it + 2])
+        diag_scores(DIAG_CUTS[it], DIAG_CUTS[it + 1])
 
     gam = mask / (valid * 0.2)
     soft = [ar_wait(0, v) for v in range(2)]
@@ -281,13 +296,13 @@
     def d_copy(q, u, ssem, rsem, dev):
         return remote(unit_ref(q, u), unit_ref(q, u), ssem, rsem, dev)
 
-    def d_core(q, s, u):
-        return d_copy(q, u, d_sc.at[s, u], dcore_recv.at[q // 2, u], core)
+    def d_core(q, u):
+        return d_copy(q, u, d_send.at[0], v_recv.at[2], core)
 
     def d_wait(q, s, u):
-        d_copy(q, u, d_sf.at[0], d_recv.at[s, u], me).wait_recv()
-
-    def grad_part(k0, size, v, acc):
+        wait_in(unit_ref(q, u), d_recv.at[s, u])
+
+    def grad_part(a_buf, v_buf, k0, size, v, acc):
         k0 = pl.multiple_of(k0, size)
         o = 1 - v
 
@@ -296,9 +311,9 @@
 
         def body(i, acc):
             n0 = pl.multiple_of(i * KDEPTH, KDEPTH)
-            a = a_ref[v, pl.ds(k0, size), pl.ds(n0, KDEPTH)].reshape(size // 8, 8, KDEPTH)
-            ao = a_ref[o, pl.ds(k0, size), pl.ds(n0, KDEPTH)].reshape(size // 8, 8, KDEPTH)
-            vo = jnp.concatenate([vbc[o, pl.ds(k0, size), :]] * (2 * wide), axis=1).reshape(size // 8, 8, KDEPTH)
+            a = a_buf[v, pl.ds(k0, size), pl.ds(n0, KDEPTH)].reshape(size // 8, 8, KDEPTH)
+            ao = a_buf[o, pl.ds(k0, size), pl.ds(n0, KDEPTH)].reshape(size // 8, 8, KDEPTH)
+            vo = jnp.concatenate([v_buf[o, pl.ds(k0, size), :]] * (2 * wide), axis=1).reshape(size // 8, 8, KDEPTH)
             g = (a * lax.rsqrt(a)) * ub[1, v, :, pl.ds(n0, KDEPTH)][None] - (ao * vo) * ub[0, o, :, pl.ds(n0, KDEPTH)][None]
             zb = zc[pl.ds(i * devs, devs), v * ROWS:(v + 1) * ROWS, :].reshape(KDEPTH, DIM)
             return acc + jnp.dot(g.reshape(size, KDEPTH).astype(BF16), zb, preferred_element_type=F32)
@@ -306,44 +321,50 @@
         return lax.fori_loop(0, SAMPLES // KDEPTH, body, acc)
 
     def grad_first(k0, size):
-        return grad_part(k0, size, 1, jnp.zeros((size, DIM), F32))
+        return grad_part(a_ref, vbc, k0, size, 1, jnp.zeros((size, DIM), F32))
 
     def grad_rest(k0, size, acc):
-        dc_ref[pl.ds(pl.multiple_of(j * COLS + k0, size), size), :] = grad_part(k0, size, 0, acc)
+        acc = grad_part(a_ref, vbc, k0, size, 0, acc)
+        dc_ref[pl.ds(pl.multiple_of(j * COLS + k0, size), size), :] = acc
+
+    def diag_units(b):
+        k0 = b * LANES
+        acc = jnp.zeros((LANES, DIM), F32)
+        for v in (1, 0):
+            acc = grad_part(ad_ref, vd, k0, LANES, v, acc)
+        dc_ref[pl.ds(pl.multiple_of(jd * COLS + DIAG * UNIT + k0, LANES), LANES), :] = acc
+        for u in range(2):
+            d_core(jd, DIAG + 2 * b + u).start()
 
     def send_own(w):
         u = unit_of(w)
-        if w < DIRECT:
-            d_copy(j, u, d_sf.at[u], d_recv.at[0, u], first).start()
-        d_core(j, 0, u).start()
+        if w < FIRST:
+            d_copy(j, u, d_send.at[1], d_recv.at[0, u], first).start()
+        d_core(j, u).start()
 
     def send_second(w):
         u = unit_of(w)
-        d_copy(j, u, d_ss.at[u], d_recv.at[1, u], second).start()
+        d_copy(j, u, d_send.at[2], d_recv.at[1, u], second).start()
+
+    def take_unit(q, s, w, direct):
+        u = unit_of(w)
+        d_wait(q, s, u)
+        if s == 0 and w < DIAG:
+            d_copy(q, u, d_send.at[3], d_recv.at[2, u], second).start()
+        if w < UNITS - direct:
+            d_copy(q, u, d_send.at[4], d_recv.at[s, u], zpart).start()
+        d_core(q, u).start()
 
     def take_first(w):
-        u = unit_of(w)
-        d_wait(jf, 0, u)
-        d_copy(jf, u, d_fs.at[u], d_recv.at[2, u], second).start()
-        if w < UNITS - DIRECT:
-            d_copy(jf, u, d_sz.at[0, u], d_recv.at[0, u], zpart).start()
-        d_core(jf, 1, u).start()
-        if w + LAG < DIRECT:
+        take_unit(jf, 0, w, FIRST)
+        if w + LAG < SECOND:
             send_second(w + LAG)
 
     def take_second(w):
-        u = unit_of(w)
-        d_wait(js, 1, u)
-        if w < UNITS - DIRECT:
-            d_copy(js, u, d_sz.at[1, u], d_recv.at[1, u], zpart).start()
-        d_core(js, 2, u).start()
+        take_unit(js, 1, w, SECOND)
 
     def take_diag(w):
-        u = unit_of(w)
-        d_wait(jd, 2, u)
-        if w < UNITS - DIRECT:
-            d_copy(jd, u, d_sz.at[2, u], d_recv.at[2, u], zpart).start()
-        d_core(jd, 3, u).start()
+        take_unit(jd, 2, w, UNITS - DIAG)
 
     def own_units(b):
         k0 = (b + par * (BLOCKS - 1 - 2 * b)) * LANES
@@ -378,9 +399,13 @@
     ips = [1.0 / p for p in ps]
     lps = [jnp.log(p) for p in ps]
     for v in range(2):
-        for o in slots:
-            buf = vall.at[v, o]
-            remote(buf, buf, v_send.at[0, 0], v_recv.at[v, o], me).wait_recv()
+        wait_in(vall.at[v, others], v_recv.at[v])
+    eye = lax.broadcasted_iota(jnp.int32, (LANES, LANES), 0) == lax.broadcasted_iota(jnp.int32, (LANES, LANES), 1)
+    for v in range(2):
+        for k0 in range(0, LOCAL, LANES):
+            row = jnp.broadcast_to(vall[v, jd, :, DIAG * UNIT + k0:DIAG * UNIT + k0 + LANES], (LANES, LANES))
+            col = jnp.sum(jnp.where(eye, row, 0.0), axis=1, keepdims=True)
+            vd[v, k0:k0 + LANES, :] = jnp.broadcast_to(col, (LANES, LANES))
     q_refs = (q1_ref, q2_ref)
     chunks = COLS // QCOLS
 
@@ -427,9 +452,7 @@
     dz2_ref[...] = dz[ROWS:]
     lpart = jnp.sum(jnp.sum(lacc, axis=0, keepdims=True), axis=1, keepdims=True)
     lbuf[j] = jnp.broadcast_to(lpart, (8, LANES))
-    l_copies = [remote(lbuf.at[j], lbuf.at[j], l_send.at[t], l_recv.at[j], dev) for t, dev in enumerate(peers)]
-    for cp in l_copies:
-        cp.start()
+    to_plane(lbuf.at[j], ar_send.at[2], l_recv.at[0])
     own_units(4)
     take_first(5)
     take_diag(1)
@@ -438,67 +461,57 @@
     own_units(5)
     take_first(7)
     take_diag(2)
+    diag_units(0)
     take_first(8)
     take_second(5)
-    own_units(6)
+    diag_units(1)
     take_first(9)
     take_diag(3)
+    diag_units(2)
     take_first(10)
     take_second(6)
-    take_diag(4)
-
-    for o in slots:
-        remote(lbuf.at[o], lbuf.at[o], l_send.at[0], l_recv.at[o], me).wait_recv()
+
+    wait_in(lbuf.at[others], l_recv.at[0])
     lsum = lbuf[0]
     for o in PEERS:
         lsum = lsum + lbuf[o]
     lzbuf[z] = lsum
-    lz_copies = [remote(lzbuf.at[z], lzbuf.at[z], lz_send.at[t], lz_recv.at[z], dev) for t, dev in enumerate(zpeers)]
-    for cp in lz_copies:
-        cp.start()
-
+    for dev in zpeers:
+        remote(lzbuf.at[z], lzbuf.at[z], ar_send.at[3], l_recv.at[1], dev).start()
+
+    diag_units(3)
+    take_first(11)
+    take_second(7)
+    own_units(6)
+    take_second(8)
+    take_second(9)
     own_units(7)
-    for w in range(7, DIRECT):
-        take_second(w)
-        take_diag(w - 2)
-    take_diag(DIRECT - 2)
-    take_diag(DIRECT - 1)
-
-    for w in reversed(range(DIRECT, UNITS)):
-        u = unit_of(w)
-        for s, q in ((0, jf), (1, js), (2, jd)):
-            d_wait(q, s, u)
-            d_core(q, s + 1, u).start()
-
-    for o in planes[1:]:
-        remote(lzbuf.at[o], lzbuf.at[o], lz_send.at[0], lz_recv.at[o], me).wait_recv()
+    take_second(10)
+    for w in reversed(range(SECOND, UNITS)):
+        for s, q, direct in ((0, jf, FIRST), (1, js, SECOND), (2, jd, UNITS - DIAG)):
+            if w >= direct:
+                u = unit_of(w)
+                d_wait(q, s, u)
+                d_core(q, u).start()
+
+    other_planes = pl.ds(0, PLANES - 1)
+    wait_in(lzbuf.at[other_planes], l_recv.at[1])
     loss = lzbuf[0]
     for o in range(1, PLANES):
         loss = loss + lzbuf[o]
     loss_ref[...] = (-loss / (2.0 * valid))[:1, :1]
 
-    @pl.loop(0, UNITS)
-    def _(u):
-        for q in range(4):
-            d_copy(2 * q + 1 - c, u, d_sf.at[0], dcore_recv.at[q, u], me).wait_recv()
-
-    for v in range(2):
-        for ph in range(ITERS + 1):
-            pending += ar_copies(ph, v)
-        pending += v_copies(v)
-    for cp in pending + l_copies + lz_copies:
-        cp.wait_send()
-    for w in range(UNITS):
-        u = unit_of(w)
-        for s in range(4):
-            d_copy(j, u, d_sc.at[s, u], dcore_recv.at[0, u], core).wait_send()
-        if w < DIRECT:
-            d_copy(j, u, d_sf.at[u], d_recv.at[0, u], first).wait_send()
-            d_copy(j, u, d_ss.at[u], d_recv.at[1, u], second).wait_send()
-            d_copy(jf, u, d_fs.at[u], d_recv.at[2, u], second).wait_send()
-        if w < UNITS - DIRECT:
-            for s in range(3):
-                d_copy(j, u, d_sz.at[s, u], d_recv.at[s, u], zpart).wait_send()
+    wait_in(dc_ref.at[pl.ds(0, PROTOS // 2), :], v_recv.at[2])
+    sent = pl.ds(0, DEVS - 1)
+    wait_out(zc.at[sent], z_send.at[0])
+    wait_out(mbuf.at[sent], z_send.at[1])
+    wait_out(rbuf.at[:, :, others], ar_send.at[0])
+    wait_out(vall.at[:, others], ar_send.at[1])
+    wait_out(lbuf.at[others], ar_send.at[2])
+    wait_out(lzbuf.at[other_planes], ar_send.at[3])
+    counts = (4 * UNITS, FIRST, SECOND, DIAG, 2 * UNITS - FIRST - SECOND + DIAG)
+    for k, units in enumerate(counts):
+        wait_out(dc_ref.at[pl.ds(0, units * UNIT), :], d_send.at[k])
 
 
 STORE = (4, 4, 1, 1, 1, 8)
@@ -540,7 +553,9 @@
                 pltpu.VMEM((DEVS, 1, LANES), F32),
                 pltpu.VMEM((PROTOS, DIM), BF16),
                 pltpu.VMEM((2, COLS, SAMPLES), F32),
+                pltpu.VMEM((2, LOCAL, SAMPLES), F32),
                 pltpu.VMEM((2, COLS, LANES), F32),
+                pltpu.VMEM((2, LOCAL, LANES), F32),
                 pltpu.VMEM((DENSE, LANES), F32),
                 pltpu.VMEM((DENSE, LANES), F32),
                 pltpu.VMEM((2, 2, 8, SAMPLES), F32),
@@ -548,12 +563,8 @@
                 pltpu.VMEM((2, PLANE, 1, COLS), F32),
                 pltpu.VMEM((PLANE, 8, LANES), F32),
                 pltpu.VMEM((PLANES, 8, LANES), F32),
-                dma((4,)), dma((DEVS - 1,)), dma((DEVS,)), dma((DEVS - 1,)), dma((DEVS,)),
-                dma((2 * ITERS + 2, PLANE - 1)), dma((2 * ITERS + 2, PLANE)),
-                dma((2, PLANE - 1)), dma((2, PLANE)),
-                dma((PLANE - 1,)), dma((PLANE,)), dma((PLANES - 1,)), dma((PLANES,)),
-                dma((3, UNITS)), dma((4, UNITS)), dma((UNITS,)), dma((UNITS,)), dma((4, UNITS)),
-                dma((UNITS,)), dma((3, UNITS)),
+                dma((4,)), dma((2,)), dma((DEVS,)), dma((PLANES,)), dma((DEVS,)), dma((PLANES,)),
+                dma((4,)), dma((2 * ITERS + 2,)), dma((3,)), dma((2,)), dma((3, UNITS)), dma((5,)),
             ],
             compiler_params=pltpu.CompilerParams(
                 collective_id=0, has_side_effects=True, vmem_limit_bytes=48 << 20),

time: 77.7 us -> 71.3 us (0.918)
  Pallas kernels: 76.9 us -> 70.5 us
    pallas_call x1, Pallas kernels: 71.5 us -> 65.1 us  [local_step(): pl.pallas_call(kernel, out_shape=[pltpu.VMEM((ROWS, PROTOS), F32), pltpu....]
where the time goes in v5:
time: 71.3 us; the launch traced here: 71.1 us
  Pallas kernels  70.5 us (99%)
    pallas_call x1, Pallas kernels, local_step(): pl.pallas_call(kernel, out_shape=[pltpu.VMEM((ROWS, PROTOS), F32), pltpu....  65.1 us
    pallas_call x1, Pallas kernels, local_step(): pl.pallas_call(store_kernel, out_shape=[jax.ShapeDtypeStruct(o.shape, o.d...  5.4 us

profile of v5, /device:TPU:0, one launch (start us, length us, event | category | flops | bytes accessed | tf_op | source)
XLA Modules:
  0.0 71.1 jit_solution(15508282164026266938)
XLA Ops:
  0.6 65.1 %shard_map.91 = (f32[64,8192]{1,0:T(8,128)S(1)}, f32[64,8192]{1,0:T(8,128)S(1)}, f32[1,1]{1,0:T(1,128)}, f32[64,256]{1,0:T(8,128)S(1)}, f32[64,256]{1,0:T(8,128)S(1)}, /*index=5*/f32[8192,256]{1,0:T(8,128)S(1)}) custom-call(bf16[64,256]{1,0:T(8,128)(2,1)} %v1_hbm.1, bf16[64,256]{1,0:T(8,128)(2,1)} %v2_hbm.1, s32[1,64]{1,0:T(1,128)} %bitcast.2, ...), custom_call_target="tpu_custom_call" | custom-call | tf_op jit(solution)/shard_map/pallas_call | solution.py:538
  65.7 5.4 %shard_map.92 = (f32[64,8192]{1,0:T(8,128)}, f32[64,8192]{1,0:T(8,128)}, f32[1,1]{1,0:T(1,128)}, f32[64,256]{1,0:T(8,128)}, f32[64,256]{1,0:T(8,128)}, /*index=5*/f32[8192,256]{1,0:T(8,128)}) custom-call(f32[64,8192]{1,0:T(8,128)S(1)} %get-tuple-element.18.refs_0_, f32[64,8192]{1,0:T(8,128)S(1)} %get-tuple-element.19.refs_1_, ...), custom_call_target="tpu_custom_call" | custom-call | tf_op jit(solution)/shard_map/pallas_call | solution.py:572

commit v6 on v5

--- a/solution.py
+++ b/solution.py
@@ -30,7 +30,7 @@
 UNITS = COLS // UNIT
 BLOCKS = COLS // LANES
 FIRST = 12
-SECOND = 11
+SECOND = 12
 DIAG = 4
 LOCAL = COLS - 2 * DIAG * UNIT
 KDEPTH = 1024
@@ -327,14 +327,13 @@
         acc = grad_part(a_ref, vbc, k0, size, 0, acc)
         dc_ref[pl.ds(pl.multiple_of(j * COLS + k0, size), size), :] = acc
 
-    def diag_units(b):
-        k0 = b * LANES
-        acc = jnp.zeros((LANES, DIM), F32)
+    def diag_units(k0, size):
+        acc = jnp.zeros((size, DIM), F32)
         for v in (1, 0):
-            acc = grad_part(ad_ref, vd, k0, LANES, v, acc)
-        dc_ref[pl.ds(pl.multiple_of(jd * COLS + DIAG * UNIT + k0, LANES), LANES), :] = acc
-        for u in range(2):
-            d_core(jd, DIAG + 2 * b + u).start()
+            acc = grad_part(ad_ref, vd, k0, size, v, acc)
+        dc_ref[pl.ds(pl.multiple_of(jd * COLS + DIAG * UNIT + k0, LANES), size), :] = acc
+        for u in range(DIAG + k0 // UNIT, DIAG + (k0 + size) // UNIT):
+            d_core(jd, u).start()
 
     def send_own(w):
         u = unit_of(w)
@@ -366,11 +365,12 @@
     def take_diag(w):
         take_unit(jd, 2, w, UNITS - DIAG)
 
-    def own_units(b):
-        k0 = (b + par * (BLOCKS - 1 - 2 * b)) * LANES
-        grad_rest(k0, LANES, grad_first(k0, LANES))
-        send_own(2 * b)
-        send_own(2 * b + 1)
+    def own_units(w, units):
+        size = units * UNIT
+        k0 = (w + par * (UNITS - units - 2 * w)) * UNIT
+        grad_rest(k0, size, grad_first(k0, size))
+        for i in range(units):
+            send_own(w + i)
 
     mu = [mask / ar_wait(ITERS, 0)]
     spread(mu[0] * gam, 0, 0)
@@ -381,9 +381,11 @@
         grad_rest(unit_of(w) * UNIT, UNIT, parts[w])
         send_own(w)
         send_second(w)
-    own_units(1)
+    own_units(2, 2)
     send_second(2)
-    own_units(2)
+    own_units(4, 2)
+    take_first(0)
+    take_second(0)
 
     sub = lax.broadcasted_iota(jnp.int32, (ROWS, LANES), 0)
     pick = lax.broadcasted_iota(jnp.int32, (ROWS, LANES), 1) == sub + ROWS * (own_slot % 2)
@@ -433,12 +435,10 @@
         return lax.fori_loop(cuts[i], cuts[i + 1], row_body, carry)
 
     carry = row_part(0, carry)
-    take_first(0)
-    take_second(0)
     carry = row_part(1, carry)
     take_first(1)
     take_second(1)
-    own_units(3)
+    own_units(6, 2)
     take_first(2)
     take_second(2)
     carry = row_part(2, carry)
@@ -453,23 +453,24 @@
     lpart = jnp.sum(jnp.sum(lacc, axis=0, keepdims=True), axis=1, keepdims=True)
     lbuf[j] = jnp.broadcast_to(lpart, (8, LANES))
     to_plane(lbuf.at[j], ar_send.at[2], l_recv.at[0])
-    own_units(4)
+    own_units(8, 2)
     take_first(5)
     take_diag(1)
     take_first(6)
     take_second(4)
-    own_units(5)
+    own_units(10, 2)
     take_first(7)
     take_diag(2)
-    diag_units(0)
+    diag_units(0, LOCAL // 2)
     take_first(8)
     take_second(5)
-    diag_units(1)
     take_first(9)
     take_diag(3)
-    diag_units(2)
+    diag_units(LOCAL // 2, LOCAL // 2)
     take_first(10)
     take_second(6)
+    take_first(11)
+    take_second(7)
 
     wait_in(lbuf.at[others], l_recv.at[0])
     lsum = lbuf[0]
@@ -479,14 +480,11 @@
     for dev in zpeers:
         remote(lzbuf.at[z], lzbuf.at[z], ar_send.at[3], l_recv.at[1], dev).start()
 
-    diag_units(3)
-    take_first(11)
-    take_second(7)
-    own_units(6)
+    own_units(12, 4)
     take_second(8)
     take_second(9)
-    own_units(7)
     take_second(10)
+    take_second(11)
     for w in reversed(range(SECOND, UNITS)):
         for s, q, direct in ((0, jf, FIRST), (1, js, SECOND), (2, jd, UNITS - DIAG)):
             if w >= direct:
@@ -499,7 +497,7 @@
     loss = lzbuf[0]
     for o in range(1, PLANES):
         loss = loss + lzbuf[o]
-    loss_ref[...] = (-loss / (2.0 * valid))[:1, :1]
+    loss_ref[...] = -loss / (2.0 * valid)
 
     wait_in(dc_ref.at[pl.ds(0, PROTOS // 2), :], v_recv.at[2])
     sent = pl.ds(0, DEVS - 1)
@@ -519,10 +517,13 @@
 
 def store_kernel(*refs):
     results = len(STORE)
-    sem = refs[2 * results]
+    one, sem = refs[2 * results:]
     copies = []
     for i, pieces in enumerate(STORE):
         src, dst = refs[i], refs[results + i]
+        if dst.shape == one.shape:
+            one[...] = src[:1, :1]
+            src = one
         rows = src.shape[0] // pieces
         for p in range(pieces):
             part = pl.ds(p * rows, rows)
@@ -540,7 +541,7 @@
             out_shape=[
                 pltpu.VMEM((ROWS, PROTOS), F32),
                 pltpu.VMEM((ROWS, PROTOS), F32),
-                pltpu.VMEM((1, 1), F32),
+                pltpu.VMEM((8, LANES), F32),
                 pltpu.VMEM((ROWS, DIM), F32),
                 pltpu.VMEM((ROWS, DIM), F32),
                 pltpu.VMEM((PROTOS, DIM), F32),
@@ -571,10 +572,10 @@
         )(view_one, view_two, valid_mask.reshape(1, ROWS), protos)
         outs = pl.pallas_call(
             store_kernel,
-            out_shape=[jax.ShapeDtypeStruct(o.shape, o.dtype) for o in outs],
+            out_shape=[jax.ShapeDtypeStruct((1, 1) if o.shape == (8, LANES) else o.shape, F32) for o in outs],
             in_specs=[pl.BlockSpec(memory_space=pltpu.VMEM)] * len(STORE),
             out_specs=[pl.BlockSpec(memory_space=pl.ANY)] * len(STORE),
-            scratch_shapes=[dma((sum(STORE),))],
+            scratch_shapes=[pltpu.VMEM((1, 1), F32), dma((sum(STORE),))],
             compiler_params=pltpu.CompilerParams(vmem_limit_bytes=4 << 20),
         )(*[pltpu.with_memory_space_constraint(o, pltpu.VMEM) for o in outs])
         q1, q2, loss, dz1, dz2, dc = outs

time: 71.3 us -> 68.1 us (0.955)
  Pallas kernels: 70.5 us -> 67.3 us
    pallas_call x1, Pallas kernels: 65.1 us -> 62.5 us  [local_step(): pl.pallas_call(kernel, out_shape=[pltpu.VMEM((ROWS, PROTOS), F32), pltpu....]
where the time goes in v6:
time: 68.1 us; the launch traced here: 67.9 us
  Pallas kernels  67.3 us (99%)
    pallas_call x1, Pallas kernels, local_step(): pl.pallas_call(kernel, out_shape=[pltpu.VMEM((ROWS, PROTOS), F32), pltpu....  62.5 us
    pallas_call x1, Pallas kernels, local_step(): pl.pallas_call(store_kernel, out_shape=[jax.ShapeDtypeStruct((1, 1) if o....  4.77 us

profile of v6, /device:TPU:0, one launch (start us, length us, event | category | flops | bytes accessed | tf_op | source)
XLA Modules:
  0.0 67.9 jit_solution(14537020486307998536)
XLA Ops:
  0.6 62.5 %shard_map.91 = (f32[64,8192]{1,0:T(8,128)S(1)}, f32[64,8192]{1,0:T(8,128)S(1)}, f32[8,128]{1,0:T(8,128)S(1)}, f32[64,256]{1,0:T(8,128)S(1)}, f32[64,256]{1,0:T(8,128)S(1)}, /*index=5*/f32[8192,256]{1,0:T(8,128)S(1)}) custom-call(bf16[64,256]{1,0:T(8,128)(2,1)} %v1_hbm.1, bf16[64,256]{1,0:T(8,128)(2,1)} %v2_hbm.1, s32[1,64]{1,0:T(1,128)} %bitcast.2, ...), custom_call_target="tpu_custom_call" | custom-call | tf_op jit(solution)/shard_map/pallas_call | solution.py:539
  63.2 4.8 %shard_map.92 = (f32[64,8192]{1,0:T(8,128)}, f32[64,8192]{1,0:T(8,128)}, f32[1,1]{1,0:T(1,128)}, f32[64,256]{1,0:T(8,128)}, f32[64,256]{1,0:T(8,128)}, /*index=5*/f32[8192,256]{1,0:T(8,128)}) custom-call(f32[64,8192]{1,0:T(8,128)S(1)} %get-tuple-element.18.refs_0_, f32[64,8192]{1,0:T(8,128)S(1)} %get-tuple-element.19.refs_1_, ...), custom_call_target="tpu_custom_call" | custom-call | tf_op jit(solution)/shard_map/pallas_call | solution.py:573

commit v7 on v6

--- a/solution.py
+++ b/solution.py
@@ -35,7 +35,6 @@
 LOCAL = COLS - 2 * DIAG * UNIT
 KDEPTH = 1024
 RCOLS = 1024
-LAG = 3
 QCOLS = 512
 GRP = 32
 LOG2E = 1.4426950408889634
@@ -47,7 +46,7 @@
 def kernel(v1_hbm, v2_hbm, mk_hbm, c_hbm,
            q1_ref, q2_ref, loss_ref, dz1_ref, dz2_ref, dc_ref,
            zc, mi, mbuf, call, a_ref, ad_ref, vbc, vd, mden, uden, ub, rbuf, vall, lbuf, lzbuf,
-           lsem, z_send, z_recv, zcore_recv, m_recv, mcore_recv, ar_send, ar_recv, v_recv, l_recv, d_recv, d_send):
+           lsem, z_send, z_recv, zcore_recv, m_send, m_recv, ar_send, ar_recv, v_recv, l_recv, d_recv, d_send):
     me = lax.axis_index("data")
     z = me // PLANE
     j = me % PLANE
@@ -98,17 +97,20 @@
     def wait_out(buf, ssem):
         remote(buf, buf, ssem, lsem.at[0], me).wait_send()
 
-    def z_copy(i, dev):
-        remote(zc.at[i], zc.at[i], z_send.at[0], z_recv.at[i], dev).start()
-        remote(mbuf.at[i], mbuf.at[i], z_send.at[1], m_recv.at[i], dev).start()
-
-    def z_core(i, p):
-        remote(zc.at[i], zc.at[i], z_send.at[0], zcore_recv.at[p], core).start()
-        remote(mbuf.at[i], mbuf.at[i], z_send.at[1], mcore_recv.at[p], core).start()
-
-    def z_wait(i):
-        wait_in(zc.at[i], z_recv.at[i])
-        wait_in(mbuf.at[i], m_recv.at[i])
+    def to_plane(buf, ssem, rsem):
+        for dev in peers:
+            remote(buf, buf, ssem, rsem, dev).start()
+
+    others = pl.ds(0, PLANE - 1)
+
+    def z_slot(p, q):
+        return zc.at[p * PLANE + c * CHIPS + q]
+
+    def z_copy(p, q, dev):
+        remote(z_slot(p, q), z_slot(p, q), z_send.at[0], z_recv.at[p * CHIPS + q], dev).start()
+
+    def z_core(p, q):
+        remote(z_slot(p, q), z_slot(p, q), z_send.at[0], zcore_recv.at[p], core).start()
 
     def row_scores(lo, hi):
         def body(i, carry):
@@ -120,26 +122,26 @@
 
         lax.fori_loop(lo, hi, body, 0)
 
-    z_copy(own_slot, first)
-    z_copy(own_slot, second)
-    for dev in zpeers:
-        z_copy(own_slot, dev)
-    z_core(own_slot, z)
+    chip = j // 2
+    for dev in (first, second, *zpeers):
+        z_copy(z, chip, dev)
+    z_core(z, chip)
+    to_plane(mbuf.at[own_slot], m_send.at[0], m_recv.at[0])
     c_copy.wait()
     row_scores(0, ROW_CUTS[0])
 
     def take(t, k, *devs):
-        i = planes[t] * PLANE + c * CHIPS + k // 2
-        z_wait(i)
+        p, q = planes[t], k // 2
+        wait_in(z_slot(p, q), z_recv.at[p * CHIPS + q])
         for dev in devs:
-            z_copy(i, dev)
-        z_core(i, planes[t])
+            z_copy(p, q, dev)
+        z_core(p, q)
 
     def take_z(t):
         take(t, j, *((first,) if t == 1 else (first, second)))
 
     def take_f(t):
-        take(t, jf, *(() if t == 1 else (second,)))
+        take(t, jf, *((second,) if t != 1 else ()))
 
     def take_s(t):
         take(t, js, *((zpart,) if t == 0 else ()))
@@ -150,7 +152,6 @@
     def take_core(t):
         part = pl.ds(planes[t] * PLANE + (1 - c) * CHIPS, CHIPS)
         wait_in(zc.at[part], zcore_recv.at[planes[t]])
-        wait_in(mbuf.at[part], mcore_recv.at[planes[t]])
 
     def scores(t, k):
         d0 = planes[t] * PLANE + k * CHIPS
@@ -184,6 +185,10 @@
     take_z(3)
     take_f(1)
     take_s(1)
+    wait_in(mbuf.at[others], m_recv.at[0])
+    block = mbuf.at[pl.ds(z * PLANE, PLANE)]
+    for dev in zpeers:
+        remote(block, block, m_send.at[1], m_recv.at[1], dev).start()
     own_scores(0)
     take_f(2)
     take_s(2)
@@ -200,12 +205,6 @@
     other_scores(2)
     other_scores(3)
 
-    def to_plane(buf, ssem, rsem):
-        for dev in peers:
-            remote(buf, buf, ssem, rsem, dev).start()
-
-    others = pl.ds(0, PLANE - 1)
-
     def ar_start(ph, v):
         to_plane(rbuf.at[ph, v, j], ar_send.at[0], ar_recv.at[2 * ph + v])
 
@@ -219,6 +218,8 @@
     ar_start(0, 0)
     ar_start(0, 1)
 
+    far = pl.ds(0, DEVS - PLANE)
+    wait_in(mbuf.at[far], m_recv.at[1])
     lane = lax.broadcasted_iota(jnp.int32, (1, LANES), 1)
     for b in range(DENSE):
         mden[pl.ds(b, 1), :] = jnp.where(lane < ROWS, mbuf[2 * b], mbuf[2 * b + 1])
@@ -356,11 +357,17 @@
 
     def take_first(w):
         take_unit(jf, 0, w, FIRST)
-        if w + LAG < SECOND:
-            send_second(w + LAG)
+        for own in (range(w + 1, w + 2) if w <= DIAG else range(2 * w - DIAG, 2 * w - DIAG + 2)):
+            if own < SECOND:
+                send_second(own)
 
     def take_second(w):
         take_unit(js, 1, w, SECOND)
+
+    def take_far(s, w):
+        u = unit_of(w)
+        d_wait((jf, js, jd)[s], s, u)
+        d_core((jf, js, jd)[s], u).start()
 
     def take_diag(w):
         take_unit(jd, 2, w, UNITS - DIAG)
@@ -380,9 +387,9 @@
     for w in range(2):
         grad_rest(unit_of(w) * UNIT, UNIT, parts[w])
         send_own(w)
-        send_second(w)
+        if w == 0:
+            send_second(w)
     own_units(2, 2)
-    send_second(2)
     own_units(4, 2)
     take_first(0)
     take_second(0)
@@ -437,16 +444,16 @@
     carry = row_part(0, carry)
     carry = row_part(1, carry)
     take_first(1)
-    take_second(1)
+    take_diag(0)
     own_units(6, 2)
     take_first(2)
-    take_second(2)
+    take_second(1)
     carry = row_part(2, carry)
     take_first(3)
-    take_diag(0)
+    take_diag(1)
     carry = row_part(3, carry)
     take_first(4)
-    take_second(3)
+    take_second(2)
     dz, lacc = row_part(4, carry)
     dz1_ref[...] = dz[:ROWS]
     dz2_ref[...] = dz[ROWS:]
@@ -455,22 +462,23 @@
     to_plane(lbuf.at[j], ar_send.at[2], l_recv.at[0])
     own_units(8, 2)
     take_first(5)
-    take_diag(1)
+    take_diag(2)
     take_first(6)
-    take_second(4)
+    take_second(3)
     own_units(10, 2)
     take_first(7)
-    take_diag(2)
+    take_diag(3)
+    for w in (15, 14):
+        take_far(0, w)
+        take_far(1, w)
     diag_units(0, LOCAL // 2)
     take_first(8)
+    take_second(4)
+    own_units(12, 4)
+    take_first(9)
     take_second(5)
-    take_first(9)
-    take_diag(3)
-    diag_units(LOCAL // 2, LOCAL // 2)
-    take_first(10)
-    take_second(6)
-    take_first(11)
-    take_second(7)
+    take_far(0, 13)
+    take_far(2, 15)
 
     wait_in(lbuf.at[others], l_recv.at[0])
     lsum = lbuf[0]
@@ -480,17 +488,20 @@
     for dev in zpeers:
         remote(lzbuf.at[z], lzbuf.at[z], ar_send.at[3], l_recv.at[1], dev).start()
 
-    own_units(12, 4)
-    take_second(8)
-    take_second(9)
-    take_second(10)
-    take_second(11)
-    for w in reversed(range(SECOND, UNITS)):
-        for s, q, direct in ((0, jf, FIRST), (1, js, SECOND), (2, jd, UNITS - DIAG)):
-            if w >= direct:
-                u = unit_of(w)
-                d_wait(q, s, u)
-                d_core(q, u).start()
+    diag_units(LOCAL // 2, LOCAL // 2)
+    take_first(10)
+    take_second(6)
+
+    take_first(11)
+    take_second(7)
+    take_far(1, 13)
+    take_far(2, 14)
+    take_far(0, 12)
+    for w in (8, 9, 10, 11):
+        take_second(w)
+    take_far(2, 13)
+    take_far(1, 12)
+    take_far(2, 12)
 
     other_planes = pl.ds(0, PLANES - 1)
     wait_in(lzbuf.at[other_planes], l_recv.at[1])
@@ -502,7 +513,8 @@
     wait_in(dc_ref.at[pl.ds(0, PROTOS // 2), :], v_recv.at[2])
     sent = pl.ds(0, DEVS - 1)
     wait_out(zc.at[sent], z_send.at[0])
-    wait_out(mbuf.at[sent], z_send.at[1])
+    wait_out(mbuf.at[others], m_send.at[0])
+    wait_out(mbuf.at[far], m_send.at[1])
     wait_out(rbuf.at[:, :, others], ar_send.at[0])
     wait_out(vall.at[:, others], ar_send.at[1])
     wait_out(lbuf.at[others], ar_send.at[2])
@@ -512,7 +524,7 @@
         wait_out(dc_ref.at[pl.ds(0, units * UNIT), :], d_send.at[k])
 
 
-STORE = (4, 4, 1, 1, 1, 8)
+STORE = (1, 1, 1, 1, 1, 2)
 
 
 def store_kernel(*refs):
@@ -564,7 +576,7 @@
                 pltpu.VMEM((2, PLANE, 1, COLS), F32),
                 pltpu.VMEM((PLANE, 8, LANES), F32),
                 pltpu.VMEM((PLANES, 8, LANES), F32),
-                dma((4,)), dma((2,)), dma((DEVS,)), dma((PLANES,)), dma((DEVS,)), dma((PLANES,)),
+                dma((4,)), dma((1,)), dma((DEVS // 2,)), dma((PLANES,)), dma((2,)), dma((2,)),
                 dma((4,)), dma((2 * ITERS + 2,)), dma((3,)), dma((2,)), dma((3, UNITS)), dma((5,)),
             ],
             compiler_params=pltpu.CompilerParams(

time: 68.1 us -> 66.9 us (0.982)
  Pallas kernels: 67.3 us -> 66.1 us
    pallas_call x1, Pallas kernels: 62.5 us -> 61.4 us  [local_step(): pl.pallas_call(kernel, out_shape=[pltpu.VMEM((ROWS, PROTOS), F32), pltpu....]
where the time goes in v7:
time: 66.9 us; the launch traced here: 66.8 us
  Pallas kernels  66.1 us (99%)
    pallas_call x1, Pallas kernels, local_step(): pl.pallas_call(kernel, out_shape=[pltpu.VMEM((ROWS, PROTOS), F32), pltpu....  61.4 us
    pallas_call x1, Pallas kernels, local_step(): pl.pallas_call(store_kernel, out_shape=[jax.ShapeDtypeStruct((1, 1) if o....  4.76 us

profile of v7, /device:TPU:0, one launch (start us, length us, event | category | flops | bytes accessed | tf_op | source)
XLA Modules:
  0.0 66.8 jit_solution(12956622260689185675)
XLA Ops:
  0.6 61.4 %shard_map.91 = (f32[64,8192]{1,0:T(8,128)S(1)}, f32[64,8192]{1,0:T(8,128)S(1)}, f32[8,128]{1,0:T(8,128)S(1)}, f32[64,256]{1,0:T(8,128)S(1)}, f32[64,256]{1,0:T(8,128)S(1)}, /*index=5*/f32[8192,256]{1,0:T(8,128)S(1)}) custom-call(bf16[64,256]{1,0:T(8,128)(2,1)} %v1_hbm.1, bf16[64,256]{1,0:T(8,128)(2,1)} %v2_hbm.1, s32[1,64]{1,0:T(1,128)} %bitcast.2, ...), custom_call_target="tpu_custom_call" | custom-call | tf_op jit(solution)/shard_map/pallas_call | solution.py:551
  62.0 4.8 %shard_map.92 = (f32[64,8192]{1,0:T(8,128)}, f32[64,8192]{1,0:T(8,128)}, f32[1,1]{1,0:T(1,128)}, f32[64,256]{1,0:T(8,128)}, f32[64,256]{1,0:T(8,128)}, /*index=5*/f32[8192,256]{1,0:T(8,128)}) custom-call(f32[64,8192]{1,0:T(8,128)S(1)} %get-tuple-element.18.refs_0_, f32[64,8192]{1,0:T(8,128)S(1)} %get-tuple-element.19.refs_1_, ...), custom_call_target="tpu_custom_call" | custom-call | tf_op jit(solution)/shard_map/pallas_call | solution.py:585

commit v8 on v7

--- a/solution.py
+++ b/solution.py
@@ -38,8 +38,8 @@
 QCOLS = 512
 GRP = 32
 LOG2E = 1.4426950408889634
-ROW_CUTS = (1, 3, 5, 7, 8)
-DIAG_CUTS = (0, 4, 5, 8)
+ROW_CUTS = (1, 3, 5, 8, 8)
+DIAG_CUTS = (0, 4, 6, 8)
 NT = (((1,), (1,)), ((), ()))
 
 

time: 66.9 us -> 66.9 us (level)
  no operation moved by 1% of the time
where the time goes in v8:
time: 66.9 us; the launch traced here: 66.8 us
  Pallas kernels  66.1 us (99%)
    pallas_call x1, Pallas kernels, local_step(): pl.pallas_call(kernel, out_shape=[pltpu.VMEM((ROWS, PROTOS), F32), pltpu....  61.4 us
    pallas_call x1, Pallas kernels, local_step(): pl.pallas_call(store_kernel, out_shape=[jax.ShapeDtypeStruct((1, 1) if o....  4.76 us

profile of v8, /device:TPU:0, one launch (start us, length us, event | category | flops | bytes accessed | tf_op | source)
XLA Modules:
  0.0 66.8 jit_solution(4239939904827948779)
XLA Ops:
  0.6 61.4 %shard_map.91 = (f32[64,8192]{1,0:T(8,128)S(1)}, f32[64,8192]{1,0:T(8,128)S(1)}, f32[8,128]{1,0:T(8,128)S(1)}, f32[64,256]{1,0:T(8,128)S(1)}, f32[64,256]{1,0:T(8,128)S(1)}, /*index=5*/f32[8192,256]{1,0:T(8,128)S(1)}) custom-call(bf16[64,256]{1,0:T(8,128)(2,1)} %v1_hbm.1, bf16[64,256]{1,0:T(8,128)(2,1)} %v2_hbm.1, s32[1,64]{1,0:T(1,128)} %bitcast.2, ...), custom_call_target="tpu_custom_call" | custom-call | tf_op jit(solution)/shard_map/pallas_call | solution.py:551
  62.0 4.8 %shard_map.92 = (f32[64,8192]{1,0:T(8,128)}, f32[64,8192]{1,0:T(8,128)}, f32[1,1]{1,0:T(1,128)}, f32[64,256]{1,0:T(8,128)}, f32[64,256]{1,0:T(8,128)}, /*index=5*/f32[8192,256]{1,0:T(8,128)}) custom-call(f32[64,8192]{1,0:T(8,128)S(1)} %get-tuple-element.18.refs_0_, f32[64,8192]{1,0:T(8,128)S(1)} %get-tuple-element.19.refs_1_, ...), custom_call_target="tpu_custom_call" | custom-call | tf_op jit(solution)/shard_map/pallas_call | solution.py:585
